TPU v7x, 32 devices: a whole 2x2x4 slice. The times are simulated.
32 devices in a mesh: seq: 8 (over z, y), ch: 4 (over x, core).
Axes of the slice: x: 2, y: 2, z: 4, core: 2. Of those that a mesh axis runs over, the one named last changes fastest.
Arguments:
- inputs: bfloat16 [8192, 768], P(('seq', 'ch')), may hold values from -6 to 6
- gain_one: float32 [768], replicated, may hold values from 0.5 to 1.5
- shift_one: float32 [768], replicated, may hold values from -1.5 to 1.5
- conv_weight: bfloat16 [3, 768, 384], P(None, None, 'ch'), may hold values from -0.125 to 0.125
- gain_two: float32 [384], P('ch'), may hold values from 0.5 to 1.5
- shift_two: float32 [384], P('ch'), may hold values from -1.5 to 1.5
- mix_weight: bfloat16 [384, 768], P('ch'), may hold values from -0.3125 to 0.3125
- head_weight: bfloat16 [768, 6956], P('ch'), may hold values from -0.21875 to 0.21875
- head_bias: float32 [6956], replicated, may hold values from -2 to 2
- species: int32 [8], replicated, may hold values from 0 to 1, as said below
- counts: int32 [8192, 5313], P(('seq', 'ch')), may hold values from 0 to 3
Outputs:
- outputs: bfloat16 [8192, 768], P(('seq', 'ch'))
- input_grad: float32 [8192, 768], P(('seq', 'ch'))
- gain_one_grad: float32 [768], replicated
- shift_one_grad: float32 [768], replicated
- conv_weight_grad: float32 [3, 768, 384], P(None, None, 'ch')
- gain_two_grad: float32 [384], P('ch')
- shift_two_grad: float32 [384], P('ch')
- mix_weight_grad: float32 [384, 768], P('ch')
- head_weight_grad: float32 [768, 6956], P(('seq', 'ch'))
- head_bias_grad: float32 [6956], replicated
Inputs may be any that keep to these rules, and one draw needn't show every extreme that they name: Each window holds one species, given by species[w]; both species occur in every draw.
All inputs are finite; a program needn't handle non-finite values.
Results may differ from a plain program's by a relative error of at most 0.014.
Values may be sent and summed in bfloat16 or wider, within the bound.
A program may use at most 192 MiB of HBM per device.

v0:
```python
import jax
import jax.numpy as jnp
from jax import lax
from jax.sharding import PartitionSpec as P

HUMAN = 5313
MOUSE = 1643
DILATION_STEP = 11
TAPS = 3
WINDOW_BINS = 1024
SHIFT = 512


norm_eps = 1e-05
contract_rows = (((0,), (0,)), ((), ()))
contract_cols = (((1,), (1,)), ((), ()))


def with_halo(cells, sides, width):
    for axis, dim in sides:
        count = lax.axis_size(axis)
        head = lax.slice_in_dim(cells, 0, width, axis=dim)
        tail = lax.slice_in_dim(cells, cells.shape[dim] - width, cells.shape[dim], axis=dim)
        cells = jnp.concatenate(
            [
                lax.ppermute(tail, axis, [(i, (i + 1) % count) for i in range(count)]),
                cells,
                lax.ppermute(head, axis, [((i + 1) % count, i) for i in range(count)]),
            ],
            axis=dim,
        )
    return cells


def window_lookup(position, total_bins):
    return jnp.mod(position - SHIFT, total_bins) // WINDOW_BINS


def gelu_grad(value, upstream):
    _, pullback = jax.vjp(jax.nn.gelu, value)
    return pullback(upstream)[0]


def poisson_grad(logits, target):
    rate = jax.nn.softplus(logits)
    return (jax.nn.sigmoid(logits) * (1.0 - target / rate)).astype(jnp.bfloat16)


def on_device(
    inputs,
    gain_one,
    shift_one,
    conv_weight,
    gain_two,
    shift_two,
    mix_weight,
    head_weight,
    head_bias,
    species,
    counts,
):
    seq_count = lax.axis_size("seq")
    ch_count = lax.axis_size("ch")
    seq_index = lax.axis_index("seq")
    ch_index = lax.axis_index("ch")
    local_rows = inputs.shape[0]
    width = inputs.shape[1]
    conv_cols = conv_weight.shape[2]
    residual_rows = local_rows * ch_count
    every_bin_list = residual_rows * seq_count
    inv_bins = 1.0 / every_bin_list
    input_f = inputs.astype(jnp.float32)
    sum_one, square_one = lax.psum(
        (jnp.sum(input_f, 0), jnp.sum(input_f * input_f, 0)), ("seq", "ch")
    )
    mean_one = sum_one * inv_bins
    scale_one = lax.rsqrt(square_one * inv_bins - mean_one * mean_one + norm_eps)
    normed_one = (input_f - mean_one) * scale_one
    pre_one = normed_one * gain_one + shift_one
    act_one = jax.nn.gelu(pre_one).astype(jnp.bfloat16)
    residual_block = lax.all_gather(act_one, "ch", axis=0, tiled=True)
    padded_input = with_halo(residual_block, (("seq", 0),), DILATION_STEP)
    bin_positions = seq_index * residual_rows + jnp.arange(residual_rows, dtype=jnp.int32)
    local_window = window_lookup(bin_positions, every_bin_list)
    fwd_masks = [
        window_lookup(bin_positions + (kernel_tap_index - 1) * DILATION_STEP, every_bin_list)
        == local_window
        for kernel_tap_index in range(TAPS)
    ]
    back_masks = [
        (
            window_lookup(bin_positions - (kernel_tap_index - 1) * DILATION_STEP, every_bin_list)
            == local_window
        ).astype(jnp.float32)[:, None]
        for kernel_tap_index in range(TAPS)
    ]
    conv_out = jnp.zeros((residual_rows, conv_cols), jnp.float32)
    for kernel_tap_index in range(TAPS):
        product = jnp.dot(
            padded_input[
                kernel_tap_index * DILATION_STEP : kernel_tap_index * DILATION_STEP + residual_rows
            ],
            conv_weight[kernel_tap_index],
            preferred_element_type=jnp.float32,
        )
        conv_out = conv_out + jnp.where(fwd_masks[kernel_tap_index][:, None], product, 0.0)
    sum_two, square_two = lax.psum((jnp.sum(conv_out, 0), jnp.sum(conv_out * conv_out, 0)), "seq")
    mean_two = sum_two * inv_bins
    scale_two = lax.rsqrt(square_two * inv_bins - mean_two * mean_two + norm_eps)
    normed_two = (conv_out - mean_two) * scale_two
    pre_two = normed_two * gain_two + shift_two
    act_two = jax.nn.gelu(pre_two).astype(jnp.bfloat16)
    branch = lax.psum_scatter(
        jnp.dot(act_two, mix_weight, preferred_element_type=jnp.float32).astype(jnp.bfloat16),
        "ch",
        scatter_dimension=0,
        tiled=True,
    ).astype(jnp.float32)
    outputs = (input_f + branch).astype(jnp.bfloat16)
    row_start = seq_index * residual_rows + ch_index * local_rows
    window_index = window_lookup(row_start, every_bin_list)
    window_ids = jnp.arange(species.shape[0], dtype=jnp.int32)
    my_species = jnp.sum(jnp.where(window_ids == window_index, species, 0))
    is_human = my_species == 0
    targets = counts.astype(jnp.float32)
    zero_human = jnp.zeros((local_rows, HUMAN), jnp.bfloat16)
    zero_mouse = jnp.zeros((local_rows, MOUSE), jnp.bfloat16)
    start_logits = (
        jnp.zeros((local_rows, HUMAN), jnp.float32),
        jnp.zeros((local_rows, MOUSE), jnp.float32),
    )
    piece = lax.all_gather(head_weight, "ch", axis=0, tiled=True)

    def human_add(unused):
        return (
            jnp.dot(outputs, piece[:, :HUMAN], preferred_element_type=jnp.float32),
            start_logits[1],
        )

    def mouse_add(unused):
        return (
            start_logits[0],
            jnp.dot(outputs, piece[:, HUMAN:], preferred_element_type=jnp.float32),
        )

    logit_sums = lax.cond(is_human, human_add, mouse_add, 0)

    def human_grads(unused):
        return (poisson_grad(logit_sums[0] + head_bias[:HUMAN], targets), zero_mouse)

    def mouse_grads(unused):
        return (zero_human, poisson_grad(logit_sums[1] + head_bias[HUMAN:], targets[:, :MOUSE]))

    grad_human, grad_mouse = lax.cond(is_human, human_grads, mouse_grads, 0)

    def back_piece(piece):

        def human_back(unused):
            return lax.dot_general(
                grad_human, piece[:, :HUMAN], contract_cols, preferred_element_type=jnp.float32
            )

        def mouse_back(unused):
            return lax.dot_general(
                grad_mouse, piece[:, HUMAN:], contract_cols, preferred_element_type=jnp.float32
            )

        return lax.cond(is_human, human_back, mouse_back, 0)

    grad_out = back_piece(lax.all_gather(head_weight, "ch", axis=0, tiled=True))

    def human_term(unused):
        part = lax.dot_general(
            outputs, grad_human, contract_rows, preferred_element_type=jnp.float32
        )
        return jnp.concatenate(
            [
                part,
                jnp.zeros(
                    (lax.axis_size(("seq", "ch")) * (width // (seq_count * ch_count)), MOUSE),
                    jnp.float32,
                ),
            ],
            1,
        )

    def mouse_term(unused):
        part = lax.dot_general(
            outputs, grad_mouse, contract_rows, preferred_element_type=jnp.float32
        )
        return jnp.concatenate(
            [
                jnp.zeros(
                    (lax.axis_size(("seq", "ch")) * (width // (seq_count * ch_count)), HUMAN),
                    jnp.float32,
                ),
                part,
            ],
            1,
        )

    head_weight_grad = lax.psum_scatter(
        lax.cond(is_human, human_term, mouse_term, 0),
        ("seq", "ch"),
        scatter_dimension=0,
        tiled=True,
    )
    bias_part = jnp.concatenate(
        [jnp.sum(grad_human.astype(jnp.float32), 0), jnp.sum(grad_mouse.astype(jnp.float32), 0)]
    )
    grad_branch = grad_out.astype(jnp.bfloat16)
    mix_piece = lax.all_gather(grad_branch, "ch", axis=0, tiled=True)
    grad_rows = lax.dot_general(
        mix_piece, mix_weight, contract_cols, preferred_element_type=jnp.float32
    )
    grad_acts = grad_rows
    mix_part = lax.dot_general(
        act_two, mix_piece, contract_rows, preferred_element_type=jnp.float32
    )
    grad_pre_two = gelu_grad(pre_two, grad_acts)
    gain_part = jnp.sum(grad_pre_two * normed_two, 0)
    shift_part = jnp.sum(grad_pre_two, 0)
    gain_two_grad, shift_two_grad = lax.psum((gain_part, shift_part), "seq")
    convolution_gradient = (
        gain_two
        * scale_two
        * (grad_pre_two - shift_two_grad * inv_bins - normed_two * gain_two_grad * inv_bins)
    ).astype(jnp.bfloat16)
    padded_gradient = with_halo(convolution_gradient, (("seq", 0),), DILATION_STEP)
    conv_part = jnp.stack(
        [
            lax.dot_general(
                padded_input[
                    kernel_tap_index * DILATION_STEP : kernel_tap_index * DILATION_STEP
                    + residual_rows
                ],
                jnp.where(
                    fwd_masks[kernel_tap_index][:, None],
                    convolution_gradient,
                    jnp.zeros_like(convolution_gradient),
                ),
                contract_rows,
                preferred_element_type=jnp.float32,
            )
            for kernel_tap_index in range(TAPS)
        ]
    )
    total = jnp.zeros((lax.axis_size("ch") * local_rows, width), jnp.float32)
    for kernel_tap_index in range(TAPS):
        grad_rows = lax.dynamic_slice_in_dim(
            padded_gradient,
            (2 - kernel_tap_index) * DILATION_STEP,
            lax.axis_size("ch") * local_rows,
            0,
        )
        product = lax.dot_general(
            grad_rows,
            conv_weight[kernel_tap_index],
            contract_cols,
            preferred_element_type=jnp.float32,
        )
        total = total + product * back_masks[kernel_tap_index]
    grad_act_one = lax.psum_scatter(
        total.astype(jnp.bfloat16), "ch", scatter_dimension=0, tiled=True
    ).astype(jnp.float32)
    grad_pre_one = gelu_grad(pre_one, grad_act_one)
    gain_one_grad, shift_one_grad, head_bias_grad = lax.psum(
        (jnp.sum(grad_pre_one * normed_one, 0), jnp.sum(grad_pre_one, 0), bias_part), ("seq", "ch")
    )
    input_grad = grad_out + gain_one * scale_one * (
        grad_pre_one - shift_one_grad * inv_bins - normed_one * gain_one_grad * inv_bins
    )
    conv_weight_grad, mix_weight_grad = lax.psum((conv_part, mix_part), "seq")
    return (
        outputs,
        input_grad,
        gain_one_grad,
        shift_one_grad,
        conv_weight_grad,
        gain_two_grad,
        shift_two_grad,
        mix_weight_grad,
        head_weight_grad,
        head_bias_grad,
    )


def solution(mesh):
    in_specs = (
        P(("seq", "ch"), None),
        P(),
        P(),
        P(None, None, "ch"),
        P("ch"),
        P("ch"),
        P("ch", None),
        P("ch", None),
        P(),
        P(),
        P(("seq", "ch"), None),
    )
    out_specs = (
        P(("seq", "ch"), None),
        P(("seq", "ch"), None),
        P(),
        P(),
        P(None, None, "ch"),
        P("ch"),
        P("ch"),
        P("ch", None),
        P(("seq", "ch"), None),
        P(),
    )
    return jax.shard_map(
        on_device, mesh=mesh, in_specs=in_specs, out_specs=out_specs, check_vma=False
    )
```

profile of v0, /device:TPU:1, one launch (start us, length us, event | category | flops | bytes accessed | tf_op | source)
XLA Modules:
  0.0 631.3 jit_solution(14036912105792922197)
XLA Ops:
  8.4 40.7 %all-reduce.4 = (f32[768]{0:T(1024)S(1)}, f32[768]{0:T(1024)S(1)}) all-reduce(f32[768]{0:T(1024)S(1)} %get-tuple-element.95, f32[768]{0:T(1024)S(1)} %get-tuple-element.94), channel_id=1, replica_groups=mesh['seq'=8,'ch'=4] {'seq','ch'}, use_global_device_ids=true, to_apply=%region_3.0 | all-reduce | flops 1536 | bytes 12288 | tf_op jit(solution)/shard_map/psum | solution.py:73
  52.1 20.8 %all-gather.4.cloned.1.call-done = bf16[1024,768]{1,0:T(8,128)(2,1)} async-done(((bf16[256,768]{1,0:T(8,128)(2,1)}), bf16[1024,768]{1,0:T(8,128)(2,1)}) %all-gather.4.cloned.1.call-update) | async-done | bytes 1572880 | tf_op jit(solution)/shard_map/all_gather | solution.py:81
  82.7 17.0 %all-reduce.6 = (f32[96]{0:T(128)S(1)}, f32[96]{0:T(128)S(1)}) all-reduce(f32[96]{0:T(128)S(1)} %get-tuple-element.93, f32[96]{0:T(128)S(1)} %get-tuple-element.92), channel_id=1, replica_groups=mesh['seq'=8,'ch'=4] {'seq'}, use_global_device_ids=true, to_apply=%region_7.8 | all-reduce | flops 192 | bytes 1536 | tf_op jit(solution)/shard_map/psum | solution.py:107
  103.8 6.1 copy.26
  110.0 5.6 convert_element_type.74
  115.6 15.3 %reduce-scatter.6.cloned.1.call-done = bf16[256,768]{1,0:T(8,128)(2,1)} async-done(((bf16[1024,768]{1,0:T(8,128)(2,1)}), bf16[256,768]{1,0:T(8,128)(2,1)}) %reduce-scatter.6.cloned.1.call-update) | async-done | bytes 393232 | tf_op jit(solution)/shard_map/reduce_scatter | solution.py:113
  132.7 72.3 %all-gather.6.cloned.1.call-done = bf16[768,6956]{1,0:T(8,128)(2,1)} async-done(((bf16[192,6956]{1,0:T(8,128)(2,1)}), bf16[768,6956]{1,0:T(8,128)(2,1)}) %all-gather.6.cloned.1.call-update) | async-done | bytes 10684432 | tf_op jit(solution)/shard_map/all_gather | solution.py:170
  205.1 5.9 conditional.4
  205.1 5.8 fusion.2
  211.0 7.6 %conditional.5 = (bf16[256,5313]{1,0:T(8,128)(2,1)S(1)}, bf16[256,1643]{1,0:T(8,128)(2,1)}) conditional(s32[]{:T(128)} %convert_element_type.73, (f32[6956]{0:T(1024)S(1)}, f32[256,1643]{0,1:T(8,128)S(1)}, f32[256,5313]{1,0:T(8,128)}) %tuple.87, (f32[6956]{0:T(1024)S(1)}, f32[256,5313]{1,0:T(8,128)S(1)}, f32[256,5313]{1,0:T(8,128)}) %tuple.88), branch_computations={%region_12.13_spmd, %region_13.14_spmd} | conditional | flops 19041792 | bytes 17040690 | solution.py:154
  211.2 6.4 %fusion.11 = bf16[256,5313]{1,0:T(8,128)(2,1)S(1)} fusion(f32[256,5313]{1,0:T(8,128)} %get-tuple-element.51, f32[256,5313]{1,0:T(8,128)S(1)} %get-tuple-element.49, f32[5313]{0:T(1024)S(1)} %slice.45), kind=kLoop, calls=%fused_computation.13 | loop fusion | flops 19041792 | bytes 13622532 | tf_op jit(solution)/shard_map/cond/branch_1_fun/convert_element_type | solution.py:46
  218.6 6.6 %conditional.6 = (f32[256,768]{1,0:T(8,128)}) conditional(s32[]{:T(128)} %convert_element_type.73, (bf16[768,6956]{1,0:T(8,128)(2,1)}, bf16[256,1643]{1,0:T(8,128)(2,1)}) %tuple.39, (bf16[768,6956]{1,0:T(8,128)(2,1)}, bf16[256,5313]{1,0:T(8,128)(2,1)S(1)}) %tuple.40), branch_computations={%region_14.15_spmd, %region_15.16_spmd} | conditional | flops 2089156608 | bytes 11764232 | solution.py:168
  218.6 6.6 %fusion.14 = f32[256,768]{1,0:T(8,128)} fusion(bf16[256,5313]{1,0:T(8,128)(2,1)S(1)} %get-tuple-element.54, bf16[768,6956]{1,0:T(8,128)(2,1)} %get-tuple-element.55), kind=kOutput, calls=%fused_computation.16 | convolution fusion | flops 2089156608 | bytes 11764224 | tf_op jit(solution)/shard_map/cond/branch_1_fun/dot_general | solution.py:159
  227.2 19.7 %all-gather.8.cloned.1.call-done = bf16[1024,768]{1,0:T(8,128)(2,1)} async-done(((bf16[256,768]{1,0:T(8,128)(2,1)}), bf16[1024,768]{1,0:T(8,128)(2,1)}) %all-gather.8.cloned.1.call-update) | async-done | bytes 1572880 | tf_op jit(solution)/shard_map/all_gather | solution.py:212
  246.9 3.0 fusion.96
  249.9 17.6 %all-reduce.5 = (f32[96]{0:T(128)S(1)}, f32[96]{0:T(128)S(1)}) all-reduce(f32[96]{0:T(128)S(1)} %get-tuple-element.91, f32[96]{0:T(128)S(1)} %get-tuple-element.90), channel_id=1, replica_groups=mesh['seq'=8,'ch'=4] {'seq'}, use_global_device_ids=true, to_apply=%region_19.20 | all-reduce | flops 192 | bytes 1536 | tf_op jit(solution)/shard_map/psum | solution.py:223
  272.8 3.2 collective-permute-done.3
  283.9 13.4 %conditional.7 = (f32[768,6956]{0,1:T(8,128)}) conditional(s32[]{:T(128)} %convert_element_type.73, (bf16[256,768]{1,0:T(8,128)(2,1)}, bf16[256,1643]{1,0:T(8,128)(2,1)}) %tuple.41, (bf16[256,768]{1,0:T(8,128)(2,1)}, bf16[256,5313]{1,0:T(8,128)(2,1)S(1)}) %tuple.42), branch_computations={%region_27.28_spmd, %region_28.29_spmd} | conditional | flops 2089156608 | bytes 57125388 | solution.py:203
  283.9 3.3 fusion.103
  287.2 10.1 %concatenate.17 = f32[768,6956]{0,1:T(8,128)} pad(f32[768,5313]{0,1:T(8,128)S(1)} %fusion.103, f32[]{:T(128)} %constant.157.clone), padding=0_0x0_1643 | pad | bytes 37690372 | tf_op jit(solution)/shard_map/cond/branch_1_fun/concatenate | solution.py:176
  297.3 21.3 %copy.28 = f32[768,6956]{1,0:T(8,128)} copy(f32[768,6956]{0,1:T(8,128)} %get-tuple-element.145) | data formatting | bytes 42737664 | tf_op jit(solution)/shard_map/cond | solution.py:203
  322.3 42.8 %all-reduce.3 = (f32[768]{0:T(1024)S(1)}, f32[768]{0:T(1024)S(1)}, f32[6956]{0:T(1024)}) all-reduce(f32[768]{0:T(1024)S(1)} %get-tuple-element.89, f32[768]{0:T(1024)S(1)} %get-tuple-element.88, f32[6956]{0:T(1024)S(1)} %pad_maximum_fusion.11), channel_id=1, replica_groups=mesh['seq'=8,'ch'=4] {'seq','ch'}, use_global_device_ids=true, to_apply=%region_24.25 | all-reduce | flops 8492 | bytes 67936 | tf_op jit(solution)/shard_map/psum | solution.py:267
  367.4 23.8 %all-reduce.10.cloned.1.call-done = (f32[3,768,96]{1,2,0:T(8,128)}, f32[96,768]{1,0:T(8,128)}) async-done(((f32[3,768,96]{1,2,0:T(8,128)}, f32[96,768]{1,0:T(8,128)}), (f32[3,768,96]{1,2,0:T(8,128)}, f32[96,768]{1,0:T(8,128)})) %all-reduce.10.cloned.1.call-update) | async-done | bytes 1179664 | tf_op jit(solution)/shard_map/psum | solution.py:273
  391.2 229.4 %reduce-scatter.10.cloned.1.call-done = f32[24,6956]{1,0:T(8,128)} async-done(((f32[768,6956]{1,0:T(8,128)}), f32[24,6956]{1,0:T(8,128)}) %reduce-scatter.10.cloned.1.call-update) | async-done | bytes 667792
  (106 shorter events, 45.0 us)
Async XLA Ops:
  7.2 92.5 %copy-start = (bf16[96,768]{1,0:T(8,128)(2,1)S(1)}, bf16[96,768]{1,0:T(8,128)(2,1)}, u32[]{:S(2)}) copy-start(bf16[96,768]{1,0:T(8,128)(2,1)} %param.25) | copy-start | bytes 442372
  7.2 72.7 %copy-start.8 = (bf16[3,768,96]{1,2,0:T(8,128)(2,1)S(1)}, bf16[3,768,96]{1,2,0:T(8,128)(2,1)}, u32[]{:S(2)}) copy-start(bf16[3,768,96]{1,2,0:T(8,128)(2,1)} %param.22) | copy-start | bytes 1327108
  7.2 65.6 %all-gather.4.cloned.1.call-start = ((), (), s32[]{:S(2)}) async-start(), calls=%async_computation.3 | async-start | bytes 1966080 | tf_op jit(solution)/shard_map/all_gather | solution.py:81
  52.0 78.9 %reduce-scatter.6.cloned.1.call-start = ((), (), s32[]{:S(2)}) async-start(), calls=%async_computation.4 | async-start | bytes 1966080 | tf_op jit(solution)/shard_map/reduce_scatter | solution.py:113
  73.6 8.3 %collective-permute-start = (bf16[11,768]{1,0:T(8,128)(2,1)S(1)}, bf16[11,768]{1,0:T(8,128)(2,1)S(1)}, u32[]{:S(2)}, u32[]{:S(2)}) collective-permute-start(bf16[11,768]{1,0:T(8,128)(2,1)S(1)} %get-tuple-element.109), channel_id=1, source_target_pairs={{0,4},{4,8},{8,12},{12,16},{16,20},{20,24},{24,28},{28,0},{1,5},{5... | collective-permute-start | bytes 50696 | tf_op jit(solution)/shard_map/ppermute | solution.py:26
  74.8 7.1 %copy-start.4 = (bf16[1024,768]{1,0:T(8,128)(2,1)S(1)}, bf16[1024,768]{1,0:T(8,128)(2,1)}, u32[]{:S(2)}) copy-start(bf16[1024,768]{1,0:T(8,128)(2,1)} %all-gather.4.cloned.1.call-done) | copy-start | bytes 4718596
  74.8 5.0 collective-permute-start.1
  81.9 17.8 %copy-start.15 = (f32[96]{0:T(128)S(1)}, f32[96]{0:T(128)}, u32[]{:S(2)}) copy-start(f32[96]{0:T(128)} %param.23) | copy-start | bytes 1156
  81.9 17.8 %copy-start.17 = (f32[96]{0:T(128)S(1)}, f32[96]{0:T(128)}, u32[]{:S(2)}) copy-start(f32[96]{0:T(128)} %param.24) | copy-start | bytes 1156
  81.9 19.7 %copy-start.19 = (bf16[11,768]{1,0:T(8,128)(2,1)}, bf16[11,768]{1,0:T(8,128)(2,1)S(1)}, u32[]{:S(2)}) copy-start(bf16[11,768]{1,0:T(8,128)(2,1)S(1)} %collective-permute-done) | copy-start | bytes 50692
  82.7 19.7 %copy-start.6 = (f32[1024,96]{0,1:T(8,128)}, f32[1024,96]{0,1:T(8,128)S(1)}, u32[]{:S(2)}) copy-start(f32[1024,96]{0,1:T(8,128)S(1)} %get-tuple-element.119) | copy-start | bytes 1179652
  101.7 103.4 %all-gather.6.cloned.1.call-start = ((), (), s32[]{:S(2)}) async-start(), calls=%async_computation.5 | async-start | bytes 13516800 | tf_op jit(solution)/shard_map/all_gather | solution.py:170
  102.4 144.5 %all-gather.8.cloned.1.call-start = ((), (), s32[]{:S(2)}) async-start(), calls=%async_computation.6 | async-start | bytes 1966080 | tf_op jit(solution)/shard_map/all_gather | solution.py:212
  110.0 20.9 %copy-start.2 = (bf16[256,768]{1,0:T(8,128)(2,1)S(1)}, bf16[256,768]{1,0:T(8,128)(2,1)}, u32[]{:S(2)}) copy-start(bf16[256,768]{1,0:T(8,128)(2,1)} %param.19) | copy-start | bytes 1179652
  205.1 5.9 copy-start.10
  227.1 93.4 %reduce-scatter.8.cloned.1.call-start = ((), (), s32[]{:S(2)}) async-start(), calls=%async_computation.7 | async-start | bytes 1966080 | tf_op jit(solution)/shard_map/reduce_scatter | solution.py:263
  267.5 5.2 copy-start.24
  269.0 3.0 collective-permute-start.2
  270.5 5.4 collective-permute-start.3
  278.2 113.1 %all-reduce.10.cloned.1.call-start = ((), (), s32[]{:S(2)}) async-start(), calls=%async_computation.9 | async-start | bytes 2359296 | tf_op jit(solution)/shard_map/psum | solution.py:273
  283.8 336.8 %reduce-scatter.10.cloned.1.call-start = ((), (), s32[]{:S(2)}) async-start(), calls=%async_computation.8 | async-start | bytes 22302720
  320.5 303.9 %copy-start.1 = (bf16[96,768]{1,0:T(8,128)(2,1)S(1)}, bf16[96,768]{1,0:T(8,128)(2,1)}, u32[]{:S(2)}) copy-start(bf16[96,768]{1,0:T(8,128)(2,1)} %param.25) | copy-start | bytes 442372
  365.2 259.3 %copy-start.13 = (f32[768]{0:T(1024)}, f32[768]{0:T(1024)S(1)}, u32[]{:S(2)}) copy-start(f32[768]{0:T(1024)S(1)} %get-tuple-element.134) | copy-start | bytes 9220
  365.2 259.3 %copy-start.14 = (f32[768]{0:T(1024)}, f32[768]{0:T(1024)S(1)}, u32[]{:S(2)}) copy-start(f32[768]{0:T(1024)S(1)} %get-tuple-element.135) | copy-start | bytes 9220
  (11 other events, 30.1 us)
Sparse Core Ops, SparseCore 0:
  52.1 20.6 all-gather.3
  101.8 29.0 reduce-scatter.5
  132.5 72.4 all-gather.5
  227.2 19.6 all-gather.7
  278.3 28.9 reduce-scatter.7
  311.2 79.9 all-reduce.9
  399.4 221.2 reduce-scatter.9
where the time goes:
time: 634 us; the launch traced here: 631 us
  waiting for transfers between devices  385 us (61%)
  blocking collectives  118 us (19%)
  local copies, waits for them, and re-layouts  43.4 us (7%)
  matrix products  34.1 us (5%)
  other arithmetic  28.7 us (5%)
  between operations  15.2 us (2%)
    unnamed x8, waiting for transfers between devices  230 us
    all_gather x1, waiting for transfers between devices, on_device(): grad_out = back_piece(lax.all_gather(head_weight, 'ch', axis=0, tiled=True))  72.3 us
    psum x1, blocking collectives, on_device(): lax.psum((jnp.sum(grad_pre_one * normed_one, 0), jnp.sum(grad_pre_one, 0)...  42.8 us
    psum x1, blocking collectives, on_device(): lax.psum((jnp.sum(input_f, 0), jnp.sum(input_f * input_f, 0)), ('seq', 'c...  40.7 us
    psum x1, waiting for transfers between devices, on_device(): conv_weight_grad, mix_weight_grad = lax.psum((conv_part, mix_part), 'seq')  23.8 us
    cond x1, local copies, waits for them, and re-layouts, on_device(): lax.cond(is_human, human_term, mouse_term, 0)  21.3 us
    all_gather x1, waiting for transfers between devices, on_device(): residual_block = lax.all_gather(act_one, 'ch', axis=0, tiled=True)  20.8 us
    all_gather x1, waiting for transfers between devices, on_device(): mix_piece = lax.all_gather(grad_branch, 'ch', axis=0, tiled=True)  19.7 us
  transfers between devices with their start and end apart: 11, of which 7 were waited for; matrix products, arithmetic and copies ran while one was open for 11% of the time, Pallas kernels for 0%

commit v1 on v0

v1 whole, which is shorter than its diff:
```python
import functools
import math
import types

import jax
import jax.numpy as jnp
from jax import lax
from jax.experimental import pallas as pl
from jax.experimental.pallas import tpu as pltpu
from jax.sharding import PartitionSpec as P

HUMAN = 5313
MOUSE = 1643
STEP = 11
TAPS = 3
WINDOW_BINS = 1024
SHIFT = 512
EPS = 1e-05

LANES = 128
NCHUNK = 7
HW = 384
MW = 128
CW = HW + MW
HALF_H = NCHUNK * HW
HALF_M = NCHUNK * MW
HALO = 32
EDGE = 16
MESH = pl.DeviceIdType.MESH
F32 = jnp.float32
BF16 = jnp.bfloat16
K0 = math.sqrt(2.0 / math.pi)
K1 = K0 * 0.044715


def nn(a, b):
    return lax.dot_general(a, b, (((1,), (0,)), ((), ())), preferred_element_type=F32)


def nt(a, b):
    return lax.dot_general(a, b, (((1,), (1,)), ((), ())), preferred_element_type=F32)


def gelu(v):
    return 0.5 * v * (1.0 + jnp.tanh(v * (K0 + K1 * (v * v))))


def gelu_slope(v):
    v2 = v * v
    th = jnp.tanh(v * (K0 + K1 * v2))
    return 0.5 * (1.0 + th) + 0.5 * v * (1.0 - th * th) * (K0 + 3.0 * K1 * v2)


def poisson_grad(logits, target):
    t = jnp.exp(-jnp.abs(logits))
    series = t * (1.0 - t * (0.5 - t * (1.0 / 3.0 - t * 0.25)))
    rate = jnp.maximum(logits, 0.0) + jnp.where(t < 0.015625, series, jnp.log(1.0 + t))
    sig = jnp.where(logits >= 0.0, 1.0, t) / (1.0 + t)
    return sig * (1.0 - target / rate)


def take(ref, sem):
    pltpu.make_async_copy(ref, ref, sem).wait()


def kernel_body(seqs, chs, fused, names, *refs):
    r = types.SimpleNamespace(**dict(zip(names, refs, strict=True)))
    r.sa, r.sb, r.ba, r.bb = ([getattr(r, f"{n}{i}") for i in range(4)] for n in ("sa", "sb", "ba", "bb"))
    S, C = seqs, chs
    s = lax.axis_index("seq")
    c = lax.axis_index("ch")
    xi = c // 2
    k = lax.rem(c, 2)
    other = c + 1 - 2 * k
    xnb = lax.rem(c + 2, C)
    xo = 1 - xi
    y = lax.rem(s, 2)
    z = s // 2
    ynb = s + 1 - 2 * y
    zb = lax.rem(z, 2)
    znb = s + 2 - 4 * zb
    dnb = znb + 1 - 2 * y
    q = lax.rem(s, 4)
    q_y = q + 1 - 2 * y
    q_z = q + 2 - 4 * zb
    q_d = q_z + 1 - 2 * y
    rows, width = r.x.shape
    n_dev = S * C
    total_bins = rows * n_dev
    inv_bins = 1.0 / total_bins
    me = s * C + c
    left = lax.rem(me + n_dev - 1, n_dev)
    right = lax.rem(me + 1, n_dev)
    left_dev = (left // C, lax.rem(left, C))
    right_dev = (right // C, lax.rem(right, C))
    row0 = me * rows
    window = lax.rem(row0 + total_bins - SHIFT, total_bins) // WINDOW_BINS
    left_same = lax.rem(row0 + total_bins - 1 + total_bins - SHIFT, total_bins) // WINDOW_BINS == window
    right_same = lax.rem(row0 + rows + total_bins - SHIFT, total_bins) // WINDOW_BINS == window
    mine_h = r.flags[0] == 0
    x_h = r.flags[1] == 0
    y_h = r.flags[2] == 0
    hp = C * LANES

    def put(src, dst, send, recv, dev):
        pltpu.make_async_remote_copy(
            src_ref=src, dst_ref=dst, send_sem=send, recv_sem=recv, device_id=dev, device_id_type=MESH
        ).start()

    barrier = pltpu.get_barrier_semaphore()

    def greet(dev):
        pl.semaphore_signal(barrier, inc=1, device_id=dev, device_id_type=MESH)

    for i in range(1, C):
        greet((s, lax.rem(c + i, C)))

    @pl.loop(1, S)
    def _(i):
        greet((lax.rem(s + i, S), c))

    greet(left_dev)
    greet(right_dev)

    W, TG = r.wbuf, r.tgb

    def human_at(half, j):
        return pl.ds(pl.multiple_of(half * HALF_H + j * HW, LANES), HW)

    def mouse_at(half, j):
        return pl.ds(pl.multiple_of(half * HALF_M + j * MW, LANES), MW)

    @pl.loop(0, NCHUNK)
    def _(j):
        pltpu.make_async_copy(r.hw.at[:, :, human_at(k, j)], W.at[j, c, :, :, pl.ds(0, HW)], r.wl.at[j]).start()
        pltpu.make_async_copy(r.mw.at[:, :, mouse_at(k, j)], W.at[j, c, :, :, pl.ds(HW, MW)], r.wl.at[j]).start()
        pltpu.make_async_copy(r.tg.at[:, human_at(k, j)], TG.at[j, k, :, pl.ds(0, HW)], r.tl.at[j]).start()
        pltpu.make_async_copy(r.tg.at[:, mouse_at(k, j)], TG.at[j, k, :, pl.ds(HW, MW)], r.tl.at[j]).start()

    CM = r.cmf
    cr = r.cm.shape[1]
    pltpu.make_async_copy(r.cm, CM.at[:, c, pl.ds(0, cr)], r.cml).start()
    for t in range(4):
        for p in range(C):
            CM[t, p, cr:LANES, :] = jnp.zeros((LANES - cr, width), BF16)

    def spread(ref, vecs):
        n = vecs[0].shape[1] // LANES
        for i, v in enumerate(vecs):
            for t in range(n):
                ref[i * n + t : i * n + t + 1, :] = v[:, t * LANES : (t + 1) * LANES]
        if ref.shape[0] > n * len(vecs):
            ref[n * len(vecs) :, :] = jnp.zeros((ref.shape[0] - n * len(vecs), LANES), F32)

    def collect(v, n):
        m = n // LANES
        return [jnp.concatenate([v[i * m + t : i * m + t + 1, :] for t in range(m)], axis=1) for i in range(2)]

    def sum_start(i):
        src, bufs = r.sa[i], r.ba[i]
        for p in range(1, C):
            put(src, bufs.at[c], r.ars.at[2 * i], r.arr.at[2 * i], (s, lax.rem(c + p, C)))
        bufs[c] = src[...]

    def sum_middle(i):
        src, bufs, far = r.sb[i], r.ba[i], r.bb[i]
        take(bufs.at[pl.ds(0, C - 1)], r.arr.at[2 * i])
        v = bufs[0]
        for p in range(1, C):
            v = v + bufs[p]
        src[...] = v

        @pl.loop(1, S)
        def _(p):
            put(src, far.at[s], r.ars.at[2 * i + 1], r.arr.at[2 * i + 1], (lax.rem(s + p, S), c))

        far[s] = v

    def sum_end(i, n):
        far = r.bb[i]
        take(far.at[pl.ds(0, S - 1)], r.arr.at[2 * i + 1])
        if S <= 8:
            v = far[0]
            for p in range(1, S):
                v = v + far[p]
        else:
            v = lax.fori_loop(1, S, lambda p, a: a + far[p], far[0])
        return v, *collect(v, n)

    BLK = 32

    def block(i, shift=0):
        return pl.ds(pl.multiple_of(i * BLK + shift, 16), BLK)

    def row_sums(terms):
        def step(i, carry):
            return tuple(a + jnp.sum(t, 0, keepdims=True) for a, t in zip(carry, terms(i), strict=True))

        return step

    zero_w = jnp.zeros((1, width), F32)

    def x_terms(i):
        v = r.x[block(i), :].astype(F32)
        return v, v * v

    s1, q1 = lax.fori_loop(0, rows // BLK, row_sums(x_terms), (zero_w, zero_w))
    spread(r.sa0, (s1, q1))

    pl.semaphore_wait(barrier, C - 1 + S - 1 + 2)

    sum_start(0)
    put(r.x.at[pl.ds(rows - HALO, HALO)], r.xl, r.hs.at[0], r.hr.at[0], right_dev)
    put(r.x.at[pl.ds(0, HALO)], r.xr, r.hs.at[1], r.hr.at[1], left_dev)
    half_w = width // 2
    put(r.cm.at[q], CM.at[q, c, pl.ds(0, cr)], r.cms.at[0], r.cmr.at[0], (s, xnb))
    put(
        r.cm.at[q_d, :, pl.ds(0, half_w)],
        CM.at[q_d, c, pl.ds(0, cr), pl.ds(0, half_w)],
        r.cms.at[1],
        r.cmr.at[1],
        (s, xnb),
    )
    put(r.cm, CM.at[:, c, pl.ds(0, cr)], r.cms.at[2], r.cmr.at[2], (s, other))
    for p in range(1, C):
        put(r.gs2, r.gsb.at[c], r.gss, r.gsr, (s, lax.rem(c + p, C)))
    r.gsb[c] = r.gs2[...]

    @pl.loop(0, NCHUNK)
    def _(j):
        put(
            r.hw.at[:, :, human_at(1 - k, j)], W.at[j, c, :, :, pl.ds(0, HW)],
            r.wps, r.wp.at[j], (s, other),
        )
        put(
            r.mw.at[:, :, mouse_at(1 - k, j)], W.at[j, c, :, :, pl.ds(HW, MW)],
            r.wps, r.wp.at[j], (s, other),
        )
        put(
            r.tg.at[:, human_at(1 - k, j)], TG.at[j, k, :, pl.ds(0, HW)],
            r.tps, r.tp.at[j], (s, other),
        )
        put(
            r.tg.at[:, mouse_at(1 - k, j)], TG.at[j, k, :, pl.ds(HW, MW)],
            r.tps, r.tp.at[j], (s, other),
        )

    HALFC = CW // 2

    def heads_along_x(j):
        for h in range(2):
            dev = (s, xo * 2 + h)
            hc = pl.multiple_of(h * HALF_H + j * HW, LANES)
            put(r.hw.at[q, :, human_at(h, j)], W.at[j, c, q, :, pl.ds(0, HW)], r.wxs, r.wx.at[j], dev)
            put(r.mw.at[q, :, mouse_at(h, j)], W.at[j, c, q, :, pl.ds(HW, MW)], r.wxs, r.wx.at[j], dev)
            put(
                r.hw.at[q_d, :, pl.ds(hc, HALFC)], W.at[j, c, q_d, :, pl.ds(0, HALFC)],
                r.wxs, r.wx.at[j], dev,
            )

    def relay_heads(j):
        take(W.at[j, pl.ds(0, 3), 0], r.wx.at[j])
        far = pl.ds(xo * 2, 2)
        put(W.at[j, far, q], W.at[j, far, q], r.wrs.at[0], r.wy.at[j], (ynb, c))
        put(W.at[j, far, q], W.at[j, far, q], r.wrs.at[1], r.wz.at[j], (znb, c))
        put(
            W.at[j, far, q, :, pl.ds(HALFC, HALFC)], W.at[j, far, q, :, pl.ds(HALFC, HALFC)],
            r.wrs.at[2], r.wd.at[j], (dnb, c),
        )

    for j in range(2):
        heads_along_x(j)

    sum_middle(0)
    _, t1, u1 = sum_end(0, width)
    mean1 = t1 * inv_bins
    scale1 = lax.rsqrt(u1 * inv_bins - mean1 * mean1 + EPS)
    gain1 = r.gs1[0:1, :]
    off1 = r.gs1[1:2, :]

    take(CM.at[0, 0, pl.ds(0, cr)], r.cmr.at[0])
    put(CM.at[q, xnb, pl.ds(0, cr)], CM.at[q, xnb, pl.ds(0, cr)], r.cms.at[3], r.cmr.at[3], (ynb, c))
    put(CM.at[q, xnb, pl.ds(0, cr)], CM.at[q, xnb, pl.ds(0, cr)], r.cms.at[4], r.cmr.at[4], (znb, c))
    second = pl.ds(half_w, half_w)
    put(
        CM.at[q, xnb, pl.ds(0, cr), second], CM.at[q, xnb, pl.ds(0, cr), second],
        r.cms.at[5], r.cmr.at[5], (dnb, c),
    )

    A = r.act

    def normed1_of(v):
        return (v - mean1) * scale1

    def act_rows(v):
        return gelu(normed1_of(v.astype(F32)) * gain1 + off1)

    @pl.loop(0, rows // BLK)
    def _(i):
        at = pl.multiple_of(i * BLK, BLK)
        A[pl.ds(at + HALO, BLK), :] = act_rows(r.x[pl.ds(at, BLK), :]).astype(BF16)

    take(r.xl, r.hr.at[0])
    A[0:HALO, :] = jnp.where(left_same, act_rows(r.xl[...]), 0.0).astype(BF16)
    take(r.xr, r.hr.at[1])
    A[rows + HALO : rows + 2 * HALO, :] = jnp.where(right_same, act_rows(r.xr[...]), 0.0).astype(BF16)

    take(CM.at[0, 0, pl.ds(0, cr), pl.ds(0, half_w)], r.cmr.at[1])
    take(CM.at[0, 0, pl.ds(0, cr)], r.cmr.at[3])
    take(CM.at[0, 0, pl.ds(0, cr)], r.cmr.at[4])
    take(CM.at[0, 0, pl.ds(0, cr), pl.ds(0, half_w)], r.cmr.at[5])
    put(CM.at[:, xnb, pl.ds(0, cr)], CM.at[:, xnb, pl.ds(0, cr)], r.cms.at[6], r.cmr.at[6], (s, other))
    take(r.cm, r.cml)
    take(CM.at[:, 0, pl.ds(0, cr)], r.cmr.at[2])
    take(CM.at[:, 0, pl.ds(0, cr)], r.cmr.at[6])

    ext = rows + 2 * EDGE
    PR = r.prod
    for t in range(TAPS):
        PR[t] = nt(A[...], CM[t].reshape(hp, width))
    CV = r.cv
    lo = HALO - EDGE
    CV[...] = (
        PR[0, lo - STEP : lo - STEP + ext, :] + PR[1, lo : lo + ext, :] + PR[2, lo + STEP : lo + STEP + ext, :]
    )
    zero_h = jnp.zeros((1, hp), F32)

    def c_terms(i):
        v = CV[block(i, EDGE), :]
        return v, v * v

    s2, q2 = lax.fori_loop(0, rows // BLK, row_sums(c_terms), (zero_h, zero_h))
    spread(r.sa1, (s2, q2))
    sum_start(1)
    for j in range(2, NCHUNK):
        heads_along_x(j)
    put(A.at[pl.ds(lo, ext)], r.actx, r.as_, r.ar_, (s, xnb))
    sum_middle(1)
    relay_heads(0)
    relay_heads(1)
    _, t2, u2 = sum_end(1, hp)
    mean2 = t2 * inv_bins
    scale2 = lax.rsqrt(u2 * inv_bins - mean2 * mean2 + EPS)
    take(r.gsb.at[pl.ds(0, C - 1)], r.gsr)
    gain2 = jnp.concatenate([r.gsb[p, 0:1, :] for p in range(C)], axis=1)
    off2 = jnp.concatenate([r.gsb[p, 1:2, :] for p in range(C)], axis=1)

    def normed2_of(v):
        return (v - mean2) * scale2

    A2 = r.a2

    @pl.loop(0, rows // BLK)
    def _(i):
        at = pl.multiple_of(i * BLK, BLK)
        v = normed2_of(CV[pl.ds(at + EDGE, BLK), :])
        A2[pl.ds(at, BLK), :] = gelu(v * gain2 + off2).astype(BF16)

    O = r.ob
    mixf = CM[3].reshape(hp, width)
    outputs = (r.x[...].astype(F32) + nn(A2[...], mixf)).astype(BF16)
    O[k] = outputs
    r.out[...] = outputs
    put(O.at[k], O.at[k], r.os, r.orr, (s, other))
    relay_heads(2)
    r.a2t[...] = A2[...].T
    take(O.at[0], r.orr)
    OT = r.ot
    OT[...] = O[...].reshape(2 * rows, width).T
    GO = r.go
    GO[...] = jnp.zeros(GO.shape, F32)
    WG, GL = r.wg, r.gl
    LG = r.lg
    HB = r.hbs
    HB[...] = jnp.zeros(HB.shape, F32)
    if fused:
        Z = S // 2

    def weight_chunk_send(j, along_x):
        if along_x:
            put(WG.at[j, :, :, xo], r.r1.at[j], r.s1.at[j], r.g1r.at[j], (s, xnb))
        else:
            put(WG.at[j, :, 1 - y], r.r1.at[j], r.s1.at[j], r.g1r.at[j], (ynb, c))

    def heads_chunk(j):
        take(W.at[j, 0], r.wl.at[j])
        take(W.at[j, 0], r.wp.at[j])
        take(W.at[j, pl.ds(0, 2), 0], r.wy.at[j])
        take(W.at[j, pl.ds(0, 2), 0], r.wz.at[j])
        take(W.at[j, pl.ds(0, 2), 0, :, pl.ds(0, HALFC)], r.wd.at[j])
        take(TG.at[j, 0], r.tl.at[j])
        take(TG.at[j, 0], r.tp.at[j])
        w = r.wsel
        w[:, MW:] = W[j, :, :, :, MW:HW].reshape(width, HW - MW)
        w[:, :MW] = jnp.where(
            mine_h, W[j, :, :, :, 0:MW].reshape(width, MW), W[j, :, :, :, HW:CW].reshape(width, MW)
        )
        wv = w[...]
        LG[...] = nn(O[...].reshape(2 * rows, width), wv)
        valid_n = jnp.where(mine_h, HUMAN - (k * HALF_H + j * HW), jnp.minimum(MOUSE - (k * HALF_M + j * MW), MW))
        valid = lax.broadcasted_iota(jnp.int32, (1, HW), 1) < valid_n
        brow = r.bias[pl.ds(k * NCHUNK + j, 1), :]
        bias = jnp.concatenate([jnp.where(mine_h, brow[:, :MW], brow[:, HW:]), brow[:, MW:HW]], axis=1)
        per = rows // BLK

        def step(i, acc):
            at = pl.multiple_of(i * BLK, BLK)
            core = i // per
            ta = pl.ds(pl.multiple_of(lax.rem(i, per) * BLK, BLK), BLK)
            lg = LG[pl.ds(at, BLK), :] + bias
            tg = TG[j, core, ta, :].astype(F32)
            tgt = jnp.concatenate([jnp.where(mine_h, tg[:, :MW], tg[:, HW:]), tg[:, MW:HW]], axis=1)
            g = jnp.where(valid, poisson_grad(lg, tgt), 0.0).astype(BF16)
            GL[pl.ds(at, BLK), :] = g
            return acc + jnp.sum(g.astype(F32), 0, keepdims=True)

        bsum = lax.fori_loop(0, 2 * per, step, jnp.zeros((1, HW), F32))
        bsum = jnp.concatenate([jnp.where(mine_h, bsum, 0.0), jnp.where(mine_h, 0.0, bsum[:, :MW])], axis=1)
        HB[...] = jnp.where(lax.broadcasted_iota(jnp.int32, HB.shape, 0) == j, bsum, HB[...])
        g = GL[...]
        GO[...] += nt(g, wv).reshape(GO.shape)
        WG[j] = nn(OT[...], g).astype(BF16).reshape(WG.shape[1:])

    @pl.loop(0, NCHUNK)
    def _(j):
        heads_chunk(j)

        @pl.when(j + 3 < NCHUNK)
        def _():
            relay_heads(j + 3)

    put(GO.at[1 - k], r.gor, r.gos, r.gorr, (s, other))
    put(r.hbs, r.hbx, r.hbsem.at[0], r.hbrem.at[0], (s, xnb))

    if fused:
        A1, R1, R2, R3 = r.acc1, r.r1, r.r2, r.r3
        two = A1.shape[3]
        own = two // 2

        def along_x(j):
            return j % 2 == 1

        def rs1(j):
            take(R1.at[j], r.g1r.at[j])
            ax = along_x(j)
            got_h = x_h if ax else y_h

            def step(i, _):
                zz, b = i // 2, lax.rem(i, 2)
                a = (WG[j, zz, b, xi] if ax else WG[j, zz, y, b]).astype(F32)
                g = R1[j, zz, b].astype(F32)
                A1[j, zz, b, :, 0:HW] = (jnp.where(mine_h, a, 0.0) + jnp.where(got_h, g, 0.0)).astype(BF16)
                A1[j, zz, b, :, HW:CW] = (
                    jnp.where(mine_h, 0.0, a[:, :MW]) + jnp.where(got_h, 0.0, g[:, :MW])
                ).astype(BF16)
                return 0

            lax.fori_loop(0, S, step, 0)
            if ax:
                put(A1.at[j, :, 1 - y], R2.at[j], r.s2.at[j], r.g2r.at[j], (ynb, c))
            else:
                put(A1.at[j, :, xo], R2.at[j], r.s2.at[j], r.g2r.at[j], (s, xnb))

        def rs2(j):
            take(R2.at[j], r.g2r.at[j])
            b = y if along_x(j) else xi
            for zz in range(Z):
                R2[j, zz] = (A1[j, zz, b].astype(F32) + R2[j, zz].astype(F32)).astype(BF16)
            R3[j, z] = R2[j, z]
            for p in range(1, Z):
                to = lax.rem(z + p, Z)
                put(R2.at[j, to], R3.at[j, z], r.s3.at[j], r.g3r.at[j], (to * 2 + y, c))

        def rs3(j):
            take(R3.at[j, pl.ds(0, Z - 1)], r.g3r.at[j])
            v = R3[j, 0].astype(F32)
            for p in range(1, Z):
                v = v + R3[j, p].astype(F32)
            r.fin[j] = v.reshape(2, own, CW)
            put(r.fin.at[j, 1 - k], r.fr.at[j], r.s4.at[j], r.g4r.at[j], (s, other))
            r.hg[k, j] = r.fin[j, k]

        def rs4(j):
            take(r.fr.at[j], r.g4r.at[j])
            r.hg[1 - k, j] = r.fr[j]

        def send(j):
            weight_chunk_send(j, along_x(j))

    else:

        def nothing(j):
            return None

        rs1 = rs2 = rs3 = rs4 = send = nothing

    G, GOR = r.gbe, r.gor
    take(GOR, r.gorr)

    @pl.loop(0, rows // BLK)
    def _(i):
        v = GO[k, block(i), :] + GOR[block(i), :]
        GOR[block(i), :] = v
        G[block(i, EDGE), :] = v.astype(BF16)

    put(G.at[pl.ds(EDGE, EDGE)], G.at[pl.ds(rows + EDGE, EDGE)], r.gs.at[0], r.gr.at[0], left_dev)
    put(G.at[pl.ds(rows, EDGE)], G.at[pl.ds(0, EDGE)], r.gs.at[1], r.gr.at[1], right_dev)
    GA, GP = r.ga, r.gp
    GA[EDGE : EDGE + rows, :] = nt(G[EDGE : EDGE + rows, :], mixf)

    def pull_two(at):
        v = normed2_of(CV[at, :])
        g = GA[at, :] * gelu_slope(v * gain2 + off2)
        GP[at, :] = g
        return g * v, g

    gs_, ss_ = lax.fori_loop(0, rows // BLK, row_sums(lambda i: pull_two(block(i, EDGE))), (zero_h, zero_h))
    spread(r.sa2, (gs_, ss_))
    sum_start(2)
    send(0)
    send(1)
    MP = r.mp
    mp = nn(r.a2t[...], G[EDGE : EDGE + rows, :]).astype(BF16).reshape(C, LANES, width)
    for p in range(C):
        MP[p % 2, p // 2] = mp[p, 0:cr, :]
    put(MP.at[1 - k], r.mr, r.mps.at[0], r.mpr.at[0], (s, other))
    sum_middle(2)
    HX = r.hbx
    take(HX, r.hbrem.at[0])
    HX[...] = HX[...] + HB[...]

    @pl.loop(1, S)
    def _(p):
        put(HX, r.hbf.at[s], r.hbsem.at[1], r.hbrem.at[1], (lax.rem(s + p, S), c))

    r.hbf[s] = HX[...]
    send(2)
    send(3)
    take(r.mr, r.mpr.at[0])
    MR = r.mr
    MR[...] = (MR[...].astype(F32) + MP[k].astype(F32)).astype(BF16)
    put(MR.at[xo], r.mx, r.mps.at[1], r.mpr.at[1], (s, xnb))
    take(r.xedge, r.gr.at[0])
    take(r.xedge, r.gr.at[1])
    for at in (0, rows + EDGE):
        GA[at : at + EDGE, :] = nt(G[at : at + EDGE, :], mixf)
        pull_two(slice(at, at + EDGE))
    total2, gsum2, ssum2 = sum_end(2, hp)
    r.tot[...] = total2
    r.g2[0:1, :] = r.tot[pl.ds(c, 1), :]
    r.g2[1:2, :] = r.tot[pl.ds(C + c, 1), :]
    coef2 = gain2 * scale2
    gmean2, smean2 = gsum2 * inv_bins, ssum2 * inv_bins
    GC, GB = r.gce, r.gcb

    def conv_grad(at):
        return (coef2 * (GP[at, :] - smean2 - normed2_of(CV[at, :]) * gmean2)).astype(BF16)

    hx = hp // 2

    @pl.loop(0, rows // BLK)
    def _(i):
        v = conv_grad(block(i, EDGE))
        GC[block(i, EDGE), :] = v.astype(F32)
        GB[0, block(i), :] = v[:, :hx]
        GB[1, block(i), :] = v[:, hx:]

    put(GB.at[xo], r.gcx, r.gbs, r.gbr, (s, xnb))
    GC[0:EDGE, :] = jnp.where(left_same, conv_grad(slice(0, EDGE)).astype(F32), 0.0)
    GC[rows + EDGE : ext, :] = jnp.where(right_same, conv_grad(slice(rows + EDGE, ext)).astype(F32), 0.0)

    G1 = r.ga1
    for t in range(TAPS):
        lo_t = EDGE + STEP - t * STEP
        part = nn(GC[lo_t : lo_t + rows, :].astype(BF16), CM[t].reshape(hp, width))
        G1[...] = part if t == 0 else G1[...] + part

    def pull_one(i):
        v = normed1_of(r.x[block(i), :].astype(F32))
        g = G1[block(i), :] * gelu_slope(v * gain1 + off1)
        G1[block(i), :] = g
        return g * v, g

    g1s, s1s = lax.fori_loop(0, rows // BLK, row_sums(pull_one), (zero_w, zero_w))
    spread(r.sa3, (g1s, s1s))
    sum_start(3)
    send(4)

    take(r.actx, r.ar_)
    take(r.gcx, r.gbr)
    ZP, CG = r.zpad, r.cg
    pad = ZP.shape[0] - rows
    ZP[0 : pad // 2, :] = jnp.zeros((pad // 2, hx), F32)
    ZP[rows + pad // 2 :, :] = jnp.zeros((pad // 2, hx), F32)
    for part in range(2):
        ZP[pad // 2 : pad // 2 + rows, :] = (GB[xi] if part == 0 else r.gcx[...]).astype(F32)
        rows_act = A[lo : lo + ext, :] if part == 0 else r.actx[...]
        for t in range(TAPS):
            lo_t = pad // 2 - EDGE + STEP - t * STEP
            v = nn(ZP[lo_t : lo_t + ext, :].T.astype(BF16), rows_act).reshape(2, LANES, width)
            CG[t] = v if part == 0 else CG[t] + v
    put(CG.at[:, 1 - k, pl.ds(0, cr)], r.cgr, r.cgs, r.cgrr, (s, other))
    sum_middle(3)
    take(r.mx, r.mpr.at[1])
    mix_sum = MR[xi].astype(F32) + r.mx[...].astype(F32)
    rs1(0)
    take(r.cgr, r.cgrr)
    if fused:
        CP, C1, C3, CF = r.cp, r.c1, r.c3, r.cf
        rp = CP.shape[2]
        weights = jnp.concatenate([CG[:, k, 0:cr, :] + r.cgr[...], mix_sum[None]], axis=0)
        CP[...] = weights.astype(BF16).reshape(CP.shape)
        put(CP.at[:, 1 - y], C1, r.ccs.at[0], r.ccr.at[0], (ynb, c))
    else:
        r.cmg[0:3] = CG[:, k, 0:cr, :] + r.cgr[...]
        r.cmg[3] = mix_sum
        r.wgo[...] = WG[...]
    total1, gsum1, ssum1 = sum_end(3, width)
    r.g1[0:1, :] = gsum1
    r.g1[1:2, :] = ssum1
    coef1 = gain1 * scale1
    gmean1, smean1 = gsum1 * inv_bins, ssum1 * inv_bins

    @pl.loop(0, rows // BLK)
    def _(i):
        v = normed1_of(r.x[block(i), :].astype(F32))
        r.ig[block(i), :] = GOR[block(i), :] + coef1 * (G1[block(i), :] - smean1 - v * gmean1)

    take(r.hbf.at[pl.ds(0, S - 1)], r.hbrem.at[1])
    HB3 = r.hb3
    HB3[...] = lax.fori_loop(1, S, lambda p, a: a + r.hbf[p], r.hbf[0])
    put(HB3, r.hbp, r.hbsem.at[2], r.hbrem.at[2], (s, other))
    r.hb[k] = HB3[...]

    if fused:
        rs1(1)
        send(5)
        send(6)
        rs2(0)
        take(C1, r.ccr.at[0])
        for zz in range(Z):
            C1[zz] = (C1[zz].astype(F32) + CP[zz, y].astype(F32)).astype(BF16)
        C3[z] = C1[z]
        for p in range(1, Z):
            to = lax.rem(z + p, Z)
            put(C1.at[to], C3.at[z], r.ccs.at[1], r.ccr.at[1], (to * 2 + y, c))
        rs1(2)
        rs2(1)
        rs3(0)
        take(C3.at[pl.ds(0, Z - 1)], r.ccr.at[1])
        v = C3[0].astype(F32)
        for p in range(1, Z):
            v = v + C3[p].astype(F32)
        CF[z, y] = v.astype(BF16)
        for p in range(1, Z):
            to = lax.rem(z + p, Z)
            put(CF.at[z, y], CF.at[z, y], r.ccs.at[2], r.ccr.at[2], (to * 2 + y, c))
        rs1(3)
        rs2(2)
        rs3(1)
        take(CF.at[pl.ds(0, Z - 1), 0], r.ccr.at[2])
        put(CF.at[:, y], CF.at[:, y], r.ccs.at[3], r.ccr.at[3], (ynb, c))
        rs1(4)
        rs2(3)
        rs3(2)
        take(CF.at[:, 0], r.ccr.at[3])
        r.cmg[...] = CF[...].reshape(r.cmg.shape).astype(F32)
        rs1(5)
        rs2(4)
        rs3(3)
        rs1(6)
        rs2(5)
        rs3(4)
        rs2(6)
        rs3(5)
        rs3(6)
        for j in range(NCHUNK):
            rs4(j)
    take(r.hbp, r.hbrem.at[2])
    r.hb[1 - k] = r.hbp[...]

    for i in range(4):
        take(r.ba[i].at[pl.ds(0, C - 1)], r.ars.at[2 * i])
        take(r.bb[i].at[pl.ds(0, S - 1)], r.ars.at[2 * i + 1])
    take(r.xl, r.hs.at[0])
    take(r.xr, r.hs.at[1])
    take(CM.at[0, 0, pl.ds(0, cr)], r.cms.at[0])
    take(CM.at[0, 0, pl.ds(0, cr), pl.ds(0, half_w)], r.cms.at[1])
    take(r.cm, r.cms.at[2])
    take(CM.at[0, 0, pl.ds(0, cr)], r.cms.at[3])
    take(CM.at[0, 0, pl.ds(0, cr)], r.cms.at[4])
    take(CM.at[0, 0, pl.ds(0, cr), pl.ds(0, half_w)], r.cms.at[5])
    take(r.cm, r.cms.at[6])
    take(r.gsb.at[pl.ds(0, C - 1)], r.gss)
    take(W.at[:, 0], r.wps)
    take(TG.at[:, 0], r.tps)
    take(W.at[:, pl.ds(0, 3), 0], r.wxs)
    take(W.at[:, pl.ds(0, 2), 0], r.wrs.at[0])
    take(W.at[:, pl.ds(0, 2), 0], r.wrs.at[1])
    take(W.at[:, 0, 0], r.wrs.at[2])
    take(r.actx, r.as_)
    take(O.at[0], r.os)
    take(GOR, r.gos)
    take(HX, r.hbsem.at[0])
    take(r.hbf.at[pl.ds(0, S - 1)], r.hbsem.at[1])
    take(HB3, r.hbsem.at[2])
    take(r.xedge, r.gs.at[0])
    take(r.xedge, r.gs.at[1])
    take(r.mr, r.mps.at[0])
    take(r.mx, r.mps.at[1])
    take(r.gcx, r.gbs)
    take(r.cgr, r.cgs)
    if fused:
        take(C1, r.ccs.at[0])
        take(C3.at[pl.ds(0, Z - 1)], r.ccs.at[1])
        take(CF.at[pl.ds(0, Z - 1), 0], r.ccs.at[2])
        take(CF.at[:, 0], r.ccs.at[3])
        for j in range(NCHUNK):
            take(R1.at[j], r.s1.at[j])
            take(R2.at[j], r.s2.at[j])
            take(R3.at[j, pl.ds(0, Z - 1)], r.s3.at[j])
            take(r.fr.at[j], r.s4.at[j])


def fused_step(seqs, chs, x, gs1, gs2, cm, bias, flags, hw, mw, tg):
    S, C = seqs, chs
    rows, width = x.shape
    n_dev = S * C
    hp = C * LANES
    cr = cm.shape[1]
    kr = hw.shape[1]
    ext = rows + 2 * EDGE
    Z = S // 2
    fused = width % (n_dev * 8) == 0 and (4 * cr) % (S * 16) == 0
    two = 2 * (width // n_dev)
    rp = 4 * cr // S
    vm = pltpu.VMEM
    dma = pltpu.SemaphoreType.DMA
    ins = dict(x=x, gs1=gs1, gs2=gs2, cm=cm, bias=bias, flags=flags, hw=hw, mw=mw, tg=tg)
    any_ins = ("hw", "mw", "tg")
    outs = dict(
        out=((rows, width), BF16),
        ig=((rows, width), F32),
        g1=((2, width), F32),
        g2=((2, LANES), F32),
        cmg=((4, cr, width), F32),
        hb=((2, 8, CW), F32),
    )
    if fused:
        outs["hg"] = ((2, NCHUNK, two // 2, CW), F32)
    else:
        outs["wgo"] = ((NCHUNK, Z, 2, 2, width // (4 * Z), HW), BF16)
    scratch = dict(
        xl=vm((HALO, width), BF16),
        xr=vm((HALO, width), BF16),
        xedge=vm((EDGE, width), BF16),
        gsb=vm((C, 8, LANES), F32),
        cmf=vm((4, C, LANES, width), BF16),
        wbuf=vm((NCHUNK, 4, 4, kr, CW), BF16),
        tgb=vm((NCHUNK, 2, rows, CW), BF16),
        act=vm((rows + 2 * HALO, width), BF16),
        actx=vm((ext, width), BF16),
        prod=vm((TAPS, rows + 2 * HALO, hp), F32),
        cv=vm((ext, hp), F32),
        a2=vm((rows, hp), BF16),
        a2t=vm((hp, rows), BF16),
        ob=vm((2, rows, width), BF16),
        ot=vm((width, 2 * rows), BF16),
        wsel=vm((width, HW), BF16),
        lg=vm((2 * rows, HW), F32),
        gl=vm((2 * rows, HW), BF16),
        wg=vm((NCHUNK, Z, 2, 2, width // (4 * Z), HW), BF16),
        go=vm((2, rows, width), F32),
        gor=vm((rows, width), F32),
        hbs=vm((8, CW), F32),
        hbx=vm((8, CW), F32),
        hbf=vm((S, 8, CW), F32),
        hb3=vm((8, CW), F32),
        hbp=vm((8, CW), F32),
        gbe=vm((ext, width), BF16),
        ga=vm((ext, hp), F32),
        gp=vm((ext, hp), F32),
        gce=vm((ext, hp), F32),
        gcb=vm((2, rows, hp // 2), BF16),
        gcx=vm((rows, hp // 2), BF16),
        ga1=vm((rows, width), F32),
        mp=vm((2, 2, cr, width), BF16),
        mr=vm((2, cr, width), BF16),
        mx=vm((cr, width), BF16),
        zpad=vm((rows + 64, hp // 2), F32),
        cg=vm((TAPS, 2, LANES, width), F32),
        cgr=vm((TAPS, cr, width), F32),
        tot=vm((8, LANES), F32),
    )
    for i, n in enumerate((16, 8, 8, 16)):
        scratch[f"sa{i}"] = vm((n, LANES), F32)
        scratch[f"sb{i}"] = vm((n, LANES), F32)
        scratch[f"ba{i}"] = vm((C, n, LANES), F32)
        scratch[f"bb{i}"] = vm((S, n, LANES), F32)
    sems = dict(
        ars=8, arr=8, hs=2, hr=2, cms=7, cmr=7, cml=0, gss=0, gsr=0, wl=7, wp=7, wx=7, wy=7, wz=7, wd=7, wps=0, wxs=0,
        wrs=3, tl=7, tp=7, tps=0, as_=0, ar_=0, os=0, gos=0, gorr=0, hbsem=3, hbrem=3, gs=2, gr=2, mps=2, mpr=2, gbs=0,
        gbr=0, cgs=0, cgrr=0, orr=0,
    )
    if fused:
        scratch.update(
            acc1=vm((NCHUNK, Z, 2, two, CW), BF16),
            r1=vm((NCHUNK, Z, 2, two, HW), BF16),
            r2=vm((NCHUNK, Z, two, CW), BF16),
            r3=vm((NCHUNK, Z, two, CW), BF16),
            fin=vm((NCHUNK, 2, two // 2, CW), F32),
            fr=vm((NCHUNK, two // 2, CW), F32),
            cp=vm((Z, 2, rp, width), BF16),
            c1=vm((Z, rp, width), BF16),
            c3=vm((Z, rp, width), BF16),
            cf=vm((Z, 2, rp, width), BF16),
        )
        sems.update(s1=7, s2=7, s3=7, s4=7, g1r=7, g2r=7, g3r=7, g4r=7, ccs=4, ccr=4)
    for name, n in sems.items():
        scratch[name] = dma((n,)) if n else dma
    names = [*ins, *outs, *scratch]

    def space(name):
        if name == "flags":
            return pl.BlockSpec(memory_space=pltpu.SMEM)
        return pl.BlockSpec(memory_space=pl.ANY if name in any_ins else pltpu.VMEM)

    got = pl.pallas_call(
        functools.partial(kernel_body, S, C, fused, names),
        out_shape=[jax.ShapeDtypeStruct(*v) for v in outs.values()],
        in_specs=[space(n) for n in ins],
        out_specs=[pl.BlockSpec(memory_space=pltpu.VMEM) for _ in outs],
        scratch_shapes=list(scratch.values()),
        compiler_params=pltpu.CompilerParams(
            collective_id=0, has_side_effects=True, vmem_limit_bytes=67_043_328
        ),
    )(*ins.values())
    return types.SimpleNamespace(**dict(zip(outs, got, strict=True))), fused


def on_device(
    inputs, gain_one, shift_one, conv_weight, gain_two, shift_two, mix_weight, head_weight, head_bias, species, counts
):
    S, C = lax.axis_size("seq"), lax.axis_size("ch")
    s, c = lax.axis_index("seq"), lax.axis_index("ch")
    rows, width = inputs.shape
    cols = conv_weight.shape[2]
    total_bins = rows * S * C
    depth = head_weight.shape[0]

    def species_at(seq, chip):
        first = (seq * C + chip * 2) * rows
        window = jnp.mod(first - SHIFT, total_bins) // WINDOW_BINS
        return jnp.sum(jnp.where(jnp.arange(species.shape[0], dtype=jnp.int32) == window, species, 0))

    xi = c // 2
    flags = jnp.stack([species_at(s, xi), species_at(s, 1 - xi), species_at(s + 1 - 2 * lax.rem(s, 2), xi)])
    gs1 = jnp.stack([gain_one, shift_one])
    gs2 = jnp.pad(jnp.stack([gain_two, shift_two]), ((0, 6), (0, LANES - cols)))
    cm = jnp.concatenate([jnp.transpose(conv_weight, (0, 2, 1)), mix_weight[None]], axis=0)
    hw = head_weight.reshape(4, depth // 4, head_weight.shape[1])
    mw = jnp.pad(hw[:, :, HUMAN:], ((0, 0), (0, 0), (0, 2 * HALF_M - MOUSE)))
    tg = jnp.pad(counts.astype(BF16), ((0, 0), (0, 2 * HALF_H - HUMAN)))
    bias = jnp.concatenate(
        [
            jnp.pad(head_bias[:HUMAN], (0, 2 * HALF_H - HUMAN)).reshape(2 * NCHUNK, HW),
            jnp.pad(head_bias[HUMAN:], (0, 2 * HALF_M - MOUSE)).reshape(2 * NCHUNK, MW),
        ],
        axis=1,
    )
    o, fused = fused_step(S, C, inputs, gs1, gs2, cm, bias, flags, hw, mw, tg)

    def whole(v):
        n = v.shape[2]
        h = jnp.transpose(v[..., :HW], (2, 0, 1, 3)).reshape(n, 2 * HALF_H)[:, :HUMAN]
        m = jnp.transpose(v[..., HW:], (2, 0, 1, 3)).reshape(n, 2 * HALF_M)[:, :MOUSE]
        return jnp.concatenate([h, m], axis=1)

    cmg = o.cmg
    if fused:
        head_weight_grad = whole(o.hg)
    else:
        part = o.wgo.reshape(NCHUNK, width, HW).astype(F32)
        human = flags[0] == 0
        part = jnp.concatenate(
            [jnp.where(human, part, 0.0), jnp.where(human, 0.0, part[..., :MW])], axis=2
        )
        core = (jnp.arange(2, dtype=jnp.int32) == lax.rem(c, 2)).reshape(2, 1, 1, 1)
        head_weight_grad = lax.psum_scatter(
            whole(jnp.where(core, part[None], 0.0)), ("seq", "ch"), scatter_dimension=0, tiled=True
        )
        cmg = lax.psum(cmg, "seq")
    head_bias_grad = whole(o.hb[:, :NCHUNK, None, :])[0]
    return (
        o.out,
        o.ig,
        o.g1[0],
        o.g1[1],
        jnp.transpose(cmg[:3], (0, 2, 1)),
        o.g2[0, :cols],
        o.g2[1, :cols],
        cmg[3],
        head_weight_grad,
        head_bias_grad,
    )


def solution(mesh):
    rows = P(("seq", "ch"), None)
    in_specs = (
        rows, P(), P(), P(None, None, "ch"), P("ch"), P("ch"), P("ch", None), P("ch", None), P(), P(), rows,
    )
    out_specs = (
        rows, rows, P(), P(), P(None, None, "ch"), P("ch"), P("ch"), P("ch", None), rows, P(),
    )
    return jax.shard_map(on_device, mesh=mesh, in_specs=in_specs, out_specs=out_specs, check_vma=False)
```

time: 634 us -> 175 us (0.28)
  waiting for transfers between devices: 385 us -> 0 us
  Pallas kernels: 0 us -> 140 us
  blocking collectives: 118 us -> 0 us
  matrix products: 34.1 us -> 0 us
  local copies, waits for them, and re-layouts: 43.4 us -> 18.6 us
  between operations: 15.2 us -> 0.89 us
  other arithmetic: 28.7 us -> 15.3 us
    unnamed x8 -> x0, waiting for transfers between devices: 230 us -> none
    pallas_call x0 -> x1, Pallas kernels: none -> 140 us  [fused_step(): pl.pallas_call(functools.partial(kernel_body, S, C, fused, names), out_sh...]
    psum x4 -> x0, blocking collectives: 118 us -> none  [the longest x1 42.8 us: on_device(): lax.psum((jnp.sum(grad_pre_one * normed_one, 0), jnp.sum(grad_pre_one, 0)...]
    all_gather x3 -> x0, waiting for transfers between devices: 113 us -> none  [the longest x1 72.3 us: on_device(): grad_out = back_piece(lax.all_gather(head_weight, 'ch', axis=0, tiled=True))]
    dot_general x15 -> x0, matrix products: 34.1 us -> none  [the longest x1 6.56 us: human_back(): lax.dot_general(grad_human, piece[:, :HUMAN], contract_cols, preferred_el...]
    psum x1 -> x0, waiting for transfers between devices: 23.8 us -> none  [on_device(): conv_weight_grad, mix_weight_grad = lax.psum((conv_part, mix_part), 'seq')]
    cond x1 -> x0, local copies, waits for them, and re-layouts: 21.3 us -> none  [on_device(): lax.cond(is_human, human_term, mouse_term, 0)]
    reduce_scatter x2 -> x0, waiting for transfers between devices: 15.3 us -> none  [the longest x1 15.3 us: on_device(): lax.psum_scatter(jnp.dot(act_two, mix_weight, preferred_element_type=jnp....]
  transfers between devices with their start and end apart: 11 -> 0, of which waited for: 7 -> 0; matrix products, arithmetic and copies ran while one was open for 11% -> 0% of each run, Pallas kernels for 0% -> 0%
where the time goes in v1:
time: 175 us
  Pallas kernels  140 us (80%)
  local copies, waits for them, and re-layouts  18.6 us (11%)
  other arithmetic  15.3 us (9%)
    pallas_call x1, Pallas kernels, fused_step(): pl.pallas_call(functools.partial(kernel_body, S, C, fused, names), out_sh...  140 us
    convert_element_type x1, other arithmetic, on_device(): tg = jnp.pad(counts.astype(BF16), ((0, 0), (0, 2 * HALF_H - HUMAN)))  4.53 us

profile of v1, /device:TPU:1, one launch (start us, length us, event | category | flops | bytes accessed | tf_op | source)
XLA Modules:
  0.0 174.8 jit_solution(17747908049453540338)
XLA Ops:
  0.8 1.3 fusion
  2.1 2.5 %pad_add_fusion.refs_5_ = s32[3]{0:T(128)} fusion(s32[1]{0:T(128)} %bitcast.7, s32[1]{0:T(128)} %bitcast.6, s32[1]{0:T(128)} %bitcast.5), kind=kLoop, calls=%fused_computation.23 | loop fusion | flops 6 | bytes 24 | tf_op jit(solution)/shard_map/stack | solution.py:857
  5.3 0.7 stack.31
  6.6 1.3 select_maximum_fusion.refs_2_
  7.9 0.8 slice.56
  8.7 0.8 slice_select_fusion
  10.1 2.0 %pad_maximum_fusion.1.refs_3_ = bf16[4,96,768]{2,1,0:T(8,128)(2,1)} fusion(bf16[1,96,768]{2,1,0:T(8,128)(2,1)} %bitcast.34, bf16[3,96,768]{2,1,0:T(8,128)(2,1)} %bitcast.33), kind=kLoop, calls=%fused_computation.2 | loop fusion | flops 294912 | bytes 1179648 | tf_op jit(solution)/shard_map/concatenate | solution.py:860
  12.0 1.3 slice.73
  13.4 0.9 pad.26.refs_7_
  14.3 4.5 %convert_element_type.13 = bf16[256,5313]{0,1:T(8,128)(2,1)} convert(s32[256,5313]{0,1:T(8,128)} %param.21) | non-fusion elementwise | flops 1360128 | bytes 8160768 | tf_op jit(solution)/shard_map/convert_element_type | solution.py:863
  18.8 3.3 %copy.25 = bf16[256,5313]{1,0:T(8,128)(2,1)S(1)} copy(bf16[256,5313]{0,1:T(8,128)(2,1)} %convert_element_type.13) | data formatting | bytes 5440512 | tf_op jit(solution)/shard_map/convert_element_type | solution.py:863
  22.1 1.7 %pad.27.refs_8_ = bf16[256,5376]{1,0:T(8,128)(2,1)} pad(bf16[256,5313]{1,0:T(8,128)(2,1)S(1)} %copy.25, bf16[]{:T(256)} %constant.89.clone.1), padding=0_0x0_63 | pad | bytes 5472770 | tf_op jit(solution)/shard_map/jit(_pad)/pad | solution.py:863
  23.8 140.0 %shard_map.186 = (bf16[256,768]{1,0:T(8,128)(2,1)}, f32[256,768]{1,0:T(8,128)}, f32[2,768]{1,0:T(2,128)}, f32[2,128]{1,0:T(2,128)}, f32[4,96,768]{2,1,0:T(8,128)...) custom-call(bf16[256,768]{1,0:T(8,128)(2,1)} %refs_0_.1, f32[2,768]{1,0:T(2,128)} %pad_maximum_fusion.3.refs_1_, ...), custom_call_target="tpu_custom_call" | custom-call | tf_op jit(solution)/shard_map/pallas_call | solution.py:828
  163.8 1.2 slice_bitcast_fusion.5
  165.1 1.4 slice_reduce_fusion
  166.4 0.8 slice_bitcast_fusion.4
  167.3 0.7 maximum_reduce_fusion
  168.0 0.9 slice_bitcast_fusion.3
  168.9 1.2 slice_bitcast_fusion.1
  170.5 1.0 pad_maximum_fusion
  171.4 0.7 slice_bitcast_fusion.2
  172.2 1.0 slice_bitcast_fusion
  173.2 0.7 copy.30
  173.9 0.9 copy.31
  (21 shorter events, 2.3 us)
Async XLA Ops:
  168.9 2.5 %copy-start = (f32[4,96,768]{2,1,0:T(8,128)S(1)}, f32[4,96,768]{2,1,0:T(8,128)}, u32[]{:S(2)}) copy-start(f32[4,96,768]{2,1,0:T(8,128)} %get-tuple-element.20) | copy-start | bytes 3538948
  170.3 3.6 %copy-start.1 = (f32[256,768]{1,0:T(8,128)S(1)}, f32[256,768]{1,0:T(8,128)}, u32[]{:S(2)}) copy-start(f32[256,768]{1,0:T(8,128)} %get-tuple-element.42) | copy-start | bytes 2359300
  170.5 2.7 %copy-start.2 = (bf16[256,768]{1,0:T(8,128)(2,1)S(1)}, bf16[256,768]{1,0:T(8,128)(2,1)}, u32[]{:S(2)}) copy-start(bf16[256,768]{1,0:T(8,128)(2,1)} %get-tuple-element.41) | copy-start | bytes 1179652

commit v2 on v1

v2 whole, which is shorter than its diff:
```python
import functools
import math
import types

import jax
import jax.numpy as jnp
from jax import lax
from jax.experimental import pallas as pl
from jax.experimental.pallas import tpu as pltpu
from jax.sharding import PartitionSpec as P

HUMAN = 5313
MOUSE = 1643
STEP = 11
TAPS = 3
WINDOW_BINS = 1024
SHIFT = 512
EPS = 1e-05

LANES = 128
NCHUNK = 7
HW = 384
MW = 128
CW = HW + MW
HALF_H = NCHUNK * HW
HALF_M = NCHUNK * MW
HALO = 32
EDGE = 16
MESH = pl.DeviceIdType.MESH
F32 = jnp.float32
BF16 = jnp.bfloat16
K0 = math.sqrt(2.0 / math.pi)
K1 = K0 * 0.044715


PLAN = {
    0: ((0, 0),),
    2: ((2, 4),),
    4: ((2, 5),),
    5: ((3, 2),),
    7: ((2, 6),),
    13: ((3, 3),),
    14: ((3, 4),),
    15: ((3, 5), (3, 6)),
    16: ((4, 0), (4, 1), (4, 2), (4, 3)),
    17: ((4, 4), (4, 5), (4, 6)),
}
LOOP = ((0, 7), (3, 4), (5, 2))
XFIRST = 3
RELAYED = 5


def nn(a, b):
    return lax.dot_general(a, b, (((1,), (0,)), ((), ())), preferred_element_type=F32)


def nt(a, b):
    return lax.dot_general(a, b, (((1,), (1,)), ((), ())), preferred_element_type=F32)


def gelu(v):
    return 0.5 * v * (1.0 + jnp.tanh(v * (K0 + K1 * (v * v))))


def gelu_slope(v):
    v2 = v * v
    th = jnp.tanh(v * (K0 + K1 * v2))
    return 0.5 * (1.0 + th) + 0.5 * v * (1.0 - th * th) * (K0 + 3.0 * K1 * v2)


def poisson_grad(logits, target):
    t = jnp.exp(-jnp.abs(logits))
    up = 1.0 + t
    series = t * (1.0 - t * (0.5 - t * (1.0 / 3.0 - t * 0.25)))
    rate = jnp.maximum(logits, 0.0) + jnp.where(t < 0.015625, series, jnp.log(up))
    return jnp.where(logits >= 0.0, 1.0, t) * (rate - target) / (up * rate)


def take(ref, sem):
    pltpu.make_async_copy(ref, ref, sem).wait()


def kernel_body(seqs, chs, fused, names, *refs):
    r = types.SimpleNamespace(**dict(zip(names, refs, strict=True)))
    r.sa, r.sb, r.ba, r.bb = ([getattr(r, f"{n}{i}") for i in range(4)] for n in ("sa", "sb", "ba", "bb"))
    S, C = seqs, chs
    s = lax.axis_index("seq")
    c = lax.axis_index("ch")
    xi = c // 2
    k = lax.rem(c, 2)
    other = c + 1 - 2 * k
    xnb = lax.rem(c + 2, C)
    xo = 1 - xi
    y = lax.rem(s, 2)
    z = s // 2
    ynb = s + 1 - 2 * y
    zb = lax.rem(z, 2)
    znb = s + 2 - 4 * zb
    dnb = znb + 1 - 2 * y
    q = lax.rem(s, 4)
    q_y = q + 1 - 2 * y
    q_z = q + 2 - 4 * zb
    q_d = q_z + 1 - 2 * y
    rows, width = r.x.shape
    n_dev = S * C
    total_bins = rows * n_dev
    inv_bins = 1.0 / total_bins
    me = s * C + c
    left = lax.rem(me + n_dev - 1, n_dev)
    right = lax.rem(me + 1, n_dev)
    left_dev = (left // C, lax.rem(left, C))
    right_dev = (right // C, lax.rem(right, C))
    row0 = me * rows
    window = lax.rem(row0 + total_bins - SHIFT, total_bins) // WINDOW_BINS
    left_same = lax.rem(row0 + total_bins - 1 + total_bins - SHIFT, total_bins) // WINDOW_BINS == window
    right_same = lax.rem(row0 + rows + total_bins - SHIFT, total_bins) // WINDOW_BINS == window

    def human_at_chip(seq, chip):
        first = (seq * C + chip * 2) * rows
        return r.species[lax.rem(first + total_bins - SHIFT, total_bins) // WINDOW_BINS] == 0

    mine_h = human_at_chip(s, xi)
    x_h = human_at_chip(s, xo)
    y_h = human_at_chip(ynb, xi)
    hp = C * LANES

    def put(src, dst, send, recv, dev):
        pltpu.make_async_remote_copy(
            src_ref=src, dst_ref=dst, send_sem=send, recv_sem=recv, device_id=dev, device_id_type=MESH
        ).start()

    barrier = pltpu.get_barrier_semaphore()

    def greet(dev):
        pl.semaphore_signal(barrier, inc=1, device_id=dev, device_id_type=MESH)

    for i in range(1, C):
        greet((s, lax.rem(c + i, C)))

    @pl.loop(1, S)
    def _(i):
        greet((lax.rem(s + i, S), c))

    greet(left_dev)
    greet(right_dev)

    W, TG = r.wbuf, r.tgb

    def human_at(half, j):
        return pl.ds(pl.multiple_of(half * HALF_H + j * HW, LANES), HW)

    def mouse_at(half, j):
        return pl.ds(pl.multiple_of(half * HALF_M + j * MW, LANES), MW)

    HV, MV, CB = r.hwv, r.mwv, r.cbuf
    load_hw = pltpu.make_async_copy(r.hw, HV, r.ld.at[0])
    load_hw.start()
    load_counts = pltpu.make_async_copy(r.counts, CB, r.ld.at[1])
    load_counts.start()
    CM, CS = r.cmf, r.cm
    cr = CS.shape[1]
    for t in range(TAPS):
        CS[t] = r.cw[t]
        CM[t, c, 0:cr, :] = r.cw[t]
    CS[TAPS] = r.mix[...]
    CM[TAPS, c, 0:cr, :] = r.mix[...]
    for t in range(4):
        for p in range(C):
            CM[t, p, cr:LANES, :] = jnp.zeros((LANES - cr, width), BF16)
    r.gs2[...] = jnp.zeros(r.gs2.shape, F32)
    r.gs2[0:1, 0:cr] = r.gain2[...].reshape(1, cr)
    r.gs2[1:2, 0:cr] = r.shift2[...].reshape(1, cr)
    M0 = HUMAN // LANES * LANES
    OFF = HUMAN - M0
    HP = r.hbpad
    tracks = HUMAN + MOUSE
    HP[:, 0:tracks] = r.bias[...].reshape(1, tracks)
    HP[:, tracks:] = jnp.zeros((1, HP.shape[1] - tracks), F32)
    BR = r.bias_rows
    for m in range(2 * NCHUNK):
        BR[m : m + 1, 0:HW] = HP[:, m * HW : (m + 1) * HW]
        v = HP[:, M0 + m * LANES : M0 + (m + 2) * LANES]
        BR[m : m + 1, HW:CW] = pltpu.roll(v, 2 * LANES - OFF, 1)[:, :MW]

    def spread(ref, vecs):
        n = vecs[0].shape[1] // LANES
        for i, v in enumerate(vecs):
            for t in range(n):
                ref[i * n + t : i * n + t + 1, :] = v[:, t * LANES : (t + 1) * LANES]
        if ref.shape[0] > n * len(vecs):
            ref[n * len(vecs) :, :] = jnp.zeros((ref.shape[0] - n * len(vecs), LANES), F32)

    def collect(v, n):
        m = n // LANES
        return [jnp.concatenate([v[i * m + t : i * m + t + 1, :] for t in range(m)], axis=1) for i in range(2)]

    def sum_start(i):
        src, bufs = r.sa[i], r.ba[i]
        for p in range(1, C):
            put(src, bufs.at[c], r.ars.at[2 * i], r.arr.at[2 * i], (s, lax.rem(c + p, C)))
        bufs[c] = src[...]

    def sum_middle(i):
        src, bufs, far = r.sb[i], r.ba[i], r.bb[i]
        take(bufs.at[pl.ds(0, C - 1)], r.arr.at[2 * i])
        v = bufs[0]
        for p in range(1, C):
            v = v + bufs[p]
        src[...] = v

        @pl.loop(1, S)
        def _(p):
            put(src, far.at[s], r.ars.at[2 * i + 1], r.arr.at[2 * i + 1], (lax.rem(s + p, S), c))

        far[s] = v

    def sum_end(i, n):
        far = r.bb[i]
        take(far.at[pl.ds(0, S - 1)], r.arr.at[2 * i + 1])
        if S <= 8:
            v = far[0]
            for p in range(1, S):
                v = v + far[p]
        else:
            v = lax.fori_loop(1, S, lambda p, a: a + far[p], far[0])
        return v, *collect(v, n)

    BLK = 32

    def block(i, shift=0):
        return pl.ds(pl.multiple_of(i * BLK + shift, 16), BLK)

    def row_sums(terms):
        def step(i, carry):
            return tuple(a + jnp.sum(t, 0, keepdims=True) for a, t in zip(carry, terms(i), strict=True))

        return step

    zero_w = jnp.zeros((1, width), F32)

    def x_terms(i):
        v = r.x[block(i), :].astype(F32)
        return v, v * v

    s1, q1 = lax.fori_loop(0, rows // BLK, row_sums(x_terms), (zero_w, zero_w))
    spread(r.sa0, (s1, q1))
    load_hw.wait()
    full = (tracks - M0) // LANES - 1
    for p in range(4):
        for m in range(2 * NCHUNK):
            if m < full:
                v = HV[p, :, M0 + m * LANES : M0 + (m + 2) * LANES].astype(F32)
                v = pltpu.roll(v, 2 * LANES - OFF, 1)[:, :MW]
            elif M0 + m * LANES < tracks:
                v = HV[p, :, M0 + m * LANES : min(tracks, M0 + (m + 2) * LANES)].astype(F32)
                v = jnp.concatenate([v, jnp.zeros((v.shape[0], 2 * LANES - v.shape[1]), F32)], axis=1)
                v = pltpu.roll(v, 2 * LANES - OFF, 1)[:, :MW]
            else:
                v = jnp.zeros((HV.shape[1], MW), F32)
            MV[p, :, m * MW : (m + 1) * MW] = v.astype(BF16)

    @pl.loop(0, NCHUNK)
    def _(j):
        pltpu.make_async_copy(HV.at[:, :, human_at(k, j)], W.at[j, c, :, :, pl.ds(0, HW)], r.wl.at[j]).start()
        pltpu.make_async_copy(MV.at[:, :, mouse_at(k, j)], W.at[j, c, :, :, pl.ds(HW, MW)], r.wl.at[j]).start()

    pl.semaphore_wait(barrier, C - 1 + S - 1 + 2)

    sum_start(0)
    put(r.x.at[pl.ds(rows - HALO, HALO)], r.xl, r.hs.at[0], r.hr.at[0], right_dev)
    put(r.x.at[pl.ds(0, HALO)], r.xr, r.hs.at[1], r.hr.at[1], left_dev)
    half_w = width // 2
    put(CS.at[q], CM.at[q, c, pl.ds(0, cr)], r.cms.at[0], r.cmr.at[0], (s, xnb))
    put(
        CS.at[q_d, :, pl.ds(0, half_w)],
        CM.at[q_d, c, pl.ds(0, cr), pl.ds(0, half_w)],
        r.cms.at[1],
        r.cmr.at[1],
        (s, xnb),
    )
    put(CS, CM.at[:, c, pl.ds(0, cr)], r.cms.at[2], r.cmr.at[2], (s, other))
    for p in range(1, C):
        put(r.gs2, r.gsb.at[c], r.gss, r.gsr, (s, lax.rem(c + p, C)))
    r.gsb[c] = r.gs2[...]

    @pl.loop(0, NCHUNK)
    def _(j):
        put(
            HV.at[:, :, human_at(1 - k, j)], W.at[j, c, :, :, pl.ds(0, HW)],
            r.wps, r.wp.at[j], (s, other),
        )
        put(
            MV.at[:, :, mouse_at(1 - k, j)], W.at[j, c, :, :, pl.ds(HW, MW)],
            r.wps, r.wp.at[j], (s, other),
        )
    HALFC = CW // 2

    def heads_along_x(j):
        for h in range(2):
            dev = (s, xo * 2 + h)
            hc = pl.multiple_of(h * HALF_H + j * HW, LANES)
            put(HV.at[q, :, human_at(h, j)], W.at[j, c, q, :, pl.ds(0, HW)], r.wxs, r.wx.at[j], dev)
            put(MV.at[q, :, mouse_at(h, j)], W.at[j, c, q, :, pl.ds(HW, MW)], r.wxs, r.wx.at[j], dev)
            put(
                HV.at[q_d, :, pl.ds(hc, HALFC)], W.at[j, c, q_d, :, pl.ds(0, HALFC)],
                r.wxs, r.wx.at[j], dev,
            )

    def relay_heads(j):
        take(W.at[j, pl.ds(0, 3), 0], r.wx.at[j])
        far = pl.ds(xo * 2, 2)
        put(W.at[j, far, q], W.at[j, far, q], r.wrs.at[0], r.wy.at[j], (ynb, c))
        put(W.at[j, far, q], W.at[j, far, q], r.wrs.at[1], r.wz.at[j], (znb, c))
        put(
            W.at[j, far, q, :, pl.ds(HALFC, HALFC)], W.at[j, far, q, :, pl.ds(HALFC, HALFC)],
            r.wrs.at[2], r.wd.at[j], (dnb, c),
        )

    for j in range(XFIRST):
        heads_along_x(j)

    def pass_weights():
        take(CM.at[0, 0, pl.ds(0, cr)], r.cmr.at[0])
        put(CM.at[q, xnb, pl.ds(0, cr)], CM.at[q, xnb, pl.ds(0, cr)], r.cms.at[3], r.cmr.at[3], (ynb, c))
        put(CM.at[q, xnb, pl.ds(0, cr)], CM.at[q, xnb, pl.ds(0, cr)], r.cms.at[4], r.cmr.at[4], (znb, c))
        second = pl.ds(half_w, half_w)
        put(
            CM.at[q, xnb, pl.ds(0, cr), second], CM.at[q, xnb, pl.ds(0, cr), second],
            r.cms.at[5], r.cmr.at[5], (dnb, c),
        )

    def targets(half, dst, j):
        at = pl.multiple_of(half * HALF_H + j * HW, 8)
        am = pl.multiple_of(half * HALF_M + j * MW, 8)
        v = CB[pl.ds(at, MW), :]
        dst[:, 0:MW] = jnp.where(mine_h, v, CB[pl.ds(am, MW), :]).astype(F32).T.astype(BF16)
        ends = (half == 1) & (j == NCHUNK - 1)

        @pl.when(ends)
        def _():
            dst[:, MW:HW] = CT[...].astype(F32).T.astype(BF16)

        @pl.when(jnp.logical_not(ends))
        def _():
            dst[:, MW:HW] = CB[pl.ds(at + MW, HW - MW), :].astype(F32).T.astype(BF16)

    load_counts.wait()
    CT = r.ctail
    whole = HUMAN - (2 * HALF_H - HW + MW)
    CT[0:whole, :] = CB[HUMAN - whole : HUMAN, :]
    CT[whole:, :] = jnp.zeros((CT.shape[0] - whole, CT.shape[1]), jnp.int32)
    sum_middle(0)
    pass_weights()

    @pl.loop(0, NCHUNK)
    def _(j):
        targets(k, TG.at[j, k], j)

    _, t1, u1 = sum_end(0, width)
    mean1 = t1 * inv_bins
    scale1 = lax.rsqrt(u1 * inv_bins - mean1 * mean1 + EPS)
    gain1 = r.gain1[...].reshape(1, width)
    off1 = r.shift1[...].reshape(1, width)

    A = r.act

    def normed1_of(v):
        return (v - mean1) * scale1

    def act_rows(v):
        return gelu(normed1_of(v.astype(F32)) * gain1 + off1)

    @pl.loop(0, rows // BLK)
    def _(i):
        at = pl.multiple_of(i * BLK, BLK)
        A[pl.ds(at + HALO, BLK), :] = act_rows(r.x[pl.ds(at, BLK), :]).astype(BF16)

    take(r.xl, r.hr.at[0])
    A[0:HALO, :] = jnp.where(left_same, act_rows(r.xl[...]), 0.0).astype(BF16)
    take(r.xr, r.hr.at[1])
    A[rows + HALO : rows + 2 * HALO, :] = jnp.where(right_same, act_rows(r.xr[...]), 0.0).astype(BF16)

    relay_heads(0)
    take(CM.at[0, 0, pl.ds(0, cr), pl.ds(0, half_w)], r.cmr.at[1])
    take(CM.at[0, 0, pl.ds(0, cr)], r.cmr.at[3])
    take(CM.at[0, 0, pl.ds(0, cr)], r.cmr.at[4])
    take(CM.at[0, 0, pl.ds(0, cr), pl.ds(0, half_w)], r.cmr.at[5])
    put(CM.at[:, xnb, pl.ds(0, cr)], CM.at[:, xnb, pl.ds(0, cr)], r.cms.at[6], r.cmr.at[6], (s, other))
    take(CM.at[:, 0, pl.ds(0, cr)], r.cmr.at[2])
    take(CM.at[:, 0, pl.ds(0, cr)], r.cmr.at[6])

    ext = rows + 2 * EDGE
    PR = r.prod
    for t in range(TAPS):
        PR[t] = nt(A[...], CM[t].reshape(hp, width))
    CV = r.cv
    lo = HALO - EDGE
    CV[...] = (
        PR[0, lo - STEP : lo - STEP + ext, :] + PR[1, lo : lo + ext, :] + PR[2, lo + STEP : lo + STEP + ext, :]
    )
    relay_heads(1)
    zero_h = jnp.zeros((1, hp), F32)

    def c_terms(i):
        v = CV[block(i, EDGE), :]
        return v, v * v

    s2, q2 = lax.fori_loop(0, rows // BLK, row_sums(c_terms), (zero_h, zero_h))
    spread(r.sa1, (s2, q2))
    sum_start(1)
    for j in range(XFIRST, NCHUNK):
        heads_along_x(j)

    @pl.loop(0, NCHUNK)
    def _(j):
        targets(1 - k, r.tgx.at[j], j)
        put(r.tgx.at[j], TG.at[j, k], r.tps, r.tp.at[j], (s, other))

    sum_middle(1)
    relay_heads(2)
    _, t2, u2 = sum_end(1, hp)
    mean2 = t2 * inv_bins
    scale2 = lax.rsqrt(u2 * inv_bins - mean2 * mean2 + EPS)
    take(r.gsb.at[pl.ds(0, C - 1)], r.gsr)
    gain2 = jnp.concatenate([r.gsb[p, 0:1, :] for p in range(C)], axis=1)
    off2 = jnp.concatenate([r.gsb[p, 1:2, :] for p in range(C)], axis=1)

    def normed2_of(v):
        return (v - mean2) * scale2

    A2 = r.a2

    @pl.loop(0, rows // BLK)
    def _(i):
        at = pl.multiple_of(i * BLK, BLK)
        v = normed2_of(CV[pl.ds(at + EDGE, BLK), :])
        A2[pl.ds(at, BLK), :] = gelu(v * gain2 + off2).astype(BF16)

    O = r.ob
    mixf = CM[3].reshape(hp, width)
    outputs = (r.x[...].astype(F32) + nn(A2[...], mixf)).astype(BF16)
    O[k] = outputs
    r.out[...] = outputs
    put(O.at[k], O.at[k], r.os, r.orr, (s, other))
    for j in range(3, RELAYED):
        relay_heads(j)
    r.a2t[...] = A2[...].T
    take(O.at[0], r.orr)
    OT = r.ot
    OT[...] = O[...].reshape(2 * rows, width).T
    GO = r.go
    GO[...] = jnp.zeros(GO.shape, F32)
    WG, GL = r.wg, r.gl
    LG = r.lg
    HB = r.hbs
    HB[...] = jnp.zeros(HB.shape, F32)
    Z = S // 2
    if fused:
        A1, R1, R2, R3 = r.acc1, r.r1, r.r2, r.r3
        two = A1.shape[3]
        own = two // 2

        def first(j, ax):
            if ax:
                put(WG.at[j, :, :, xo], R1.at[j], r.s1.at[j], r.g1r.at[j], (s, xnb))
            else:
                put(WG.at[j, :, 1 - y], R1.at[j], r.s1.at[j], r.g1r.at[j], (ynb, c))

        def second(j, ax):
            take(R1.at[j], r.g1r.at[j])
            got_h = x_h if ax else y_h

            def step(i, _):
                zz, b = i // 2, lax.rem(i, 2)
                a = (WG[j, zz, b, xi] if ax else WG[j, zz, y, b]).astype(F32)
                g = R1[j, zz, b].astype(F32)
                A1[j, zz, b, :, 0:HW] = (jnp.where(mine_h, a, 0.0) + jnp.where(got_h, g, 0.0)).astype(BF16)
                A1[j, zz, b, :, HW:CW] = (
                    jnp.where(mine_h, 0.0, a[:, :MW]) + jnp.where(got_h, 0.0, g[:, :MW])
                ).astype(BF16)
                return 0

            lax.fori_loop(0, S, step, 0)
            if ax:
                put(A1.at[j, :, 1 - y], R2.at[j], r.s2.at[j], r.g2r.at[j], (ynb, c))
            else:
                put(A1.at[j, :, xo], R2.at[j], r.s2.at[j], r.g2r.at[j], (s, xnb))

        def third(j, ax):
            take(R2.at[j], r.g2r.at[j])
            b = y if ax else xi
            for zz in range(Z):
                R2[j, zz] = (A1[j, zz, b].astype(F32) + R2[j, zz].astype(F32)).astype(BF16)
            R3[j, z] = R2[j, z]
            for p in range(1, Z):
                to = lax.rem(z + p, Z)
                put(R2.at[j, to], R3.at[j, z], r.s3.at[j], r.g3r.at[j], (to * 2 + y, c))

        def last(j):
            take(R3.at[j, pl.ds(0, Z - 1)], r.g3r.at[j])
            v = R3[j, 0].astype(F32)
            for p in range(1, Z):
                v = v + R3[j, p].astype(F32)
            r.fin[j] = v.reshape(2, own, CW)
            put(r.fin.at[j, 1 - k], r.fr.at[j], r.s4.at[j], r.g4r.at[j], (s, other))

        def either(step, j):
            @pl.when(lax.rem(j, 2) == 1)
            def _():
                step(j, True)

            @pl.when(lax.rem(j, 2) == 0)
            def _():
                step(j, False)

    def heads_chunk(j):
        take(W.at[j, 0], r.wl.at[j])
        take(W.at[j, 0], r.wp.at[j])
        take(W.at[j, pl.ds(0, 2), 0], r.wy.at[j])
        take(W.at[j, pl.ds(0, 2), 0], r.wz.at[j])
        take(W.at[j, pl.ds(0, 2), 0, :, pl.ds(0, HALFC)], r.wd.at[j])
        take(TG.at[j, 0], r.tp.at[j])
        w = r.wsel
        w[:, MW:] = W[j, :, :, :, MW:HW].reshape(width, HW - MW)
        w[:, :MW] = jnp.where(
            mine_h, W[j, :, :, :, 0:MW].reshape(width, MW), W[j, :, :, :, HW:CW].reshape(width, MW)
        )
        wv = w[...]
        LG[...] = nn(O[...].reshape(2 * rows, width), wv)
        valid_n = jnp.where(mine_h, HUMAN - (k * HALF_H + j * HW), jnp.minimum(MOUSE - (k * HALF_M + j * MW), MW))
        valid = lax.broadcasted_iota(jnp.int32, (1, HW), 1) < valid_n
        brow = BR[pl.ds(k * NCHUNK + j, 1), :]
        bias = jnp.concatenate([jnp.where(mine_h, brow[:, :MW], brow[:, HW:]), brow[:, MW:HW]], axis=1)
        per = rows // BLK

        def step(i, acc):
            at = pl.multiple_of(i * BLK, BLK)
            core = i // per
            ta = pl.ds(pl.multiple_of(lax.rem(i, per) * BLK, BLK), BLK)
            lg = LG[pl.ds(at, BLK), :] + bias
            tgt = TG[j, core, ta, :].astype(F32)
            g = jnp.where(valid, poisson_grad(lg, tgt), 0.0).astype(BF16)
            GL[pl.ds(at, BLK), :] = g
            return acc + jnp.sum(g.astype(F32).reshape(BLK // 8, 8, HW), 0)

        bsum = jnp.sum(lax.fori_loop(0, 2 * per, step, jnp.zeros((8, HW), F32)), 0, keepdims=True)
        bsum = jnp.concatenate([jnp.where(mine_h, bsum, 0.0), jnp.where(mine_h, 0.0, bsum[:, :MW])], axis=1)
        HB[...] = jnp.where(lax.broadcasted_iota(jnp.int32, HB.shape, 0) == j, bsum, HB[...])
        g = GL[...]
        GO[...] += nt(g, wv).reshape(GO.shape)
        WG[j] = nn(OT[...], g).astype(BF16).reshape(WG.shape[1:])

    act_rows_out = functools.partial(put, A.at[pl.ds(lo, ext)], r.actx, r.as_, r.ar_, (s, xnb))

    def at(slot):
        for stage, j in PLAN.get(slot, ()):
            if stage == 0:
                act_rows_out()
            elif fused:
                (first, second, third)[stage - 1](j, j % 2 == 1) if stage < 4 else last(j)

    at(0)

    @pl.loop(0, NCHUNK)
    def _(j):
        heads_chunk(j)

        @pl.when(j + RELAYED < NCHUNK)
        def _():
            relay_heads(j + RELAYED)

        if fused:
            for stage, step in ((1, first), (2, second), (3, third)):
                lag, count = LOOP[stage - 1]
                if count > 0:

                    @pl.when((j >= lag) & (j - lag < count))
                    def _(step=step, lag=lag):
                        either(step, j - lag)

    put(GO.at[1 - k], r.gor, r.gos, r.gorr, (s, other))
    put(r.hbs, r.hbx, r.hbsem.at[0], r.hbrem.at[0], (s, xnb))
    at(1)

    if fused:
        CP, C1, C3, CF = ([getattr(r, f"{n}{i}") for i in range(3)] for n in ("cp", "c1", "c3", "cf"))

        def lanes(b):
            return pl.ds(pl.multiple_of(b * half_w, LANES), half_w)

        def weights_out(i, v):
            CP[i][...] = v.astype(BF16).reshape(CP[i].shape)
            put(CP[i].at[:, :, lanes(1 - y)], C1[i], r.ccs.at[4 * i], r.ccr.at[4 * i], (ynb, c))

        def weights_along_z(i):
            take(C1[i], r.ccr.at[4 * i])
            C1[i][...] = (C1[i][...].astype(F32) + CP[i][:, :, lanes(y)].astype(F32)).astype(BF16)
            C3[i][z] = C1[i][z]
            for p in range(1, Z):
                to = lax.rem(z + p, Z)
                put(C1[i].at[to], C3[i].at[z], r.ccs.at[4 * i + 1], r.ccr.at[4 * i + 1], (to * 2 + y, c))

        def weights_back_z(i):
            take(C3[i].at[pl.ds(0, Z - 1)], r.ccr.at[4 * i + 1])
            v = C3[i][0].astype(F32)
            for p in range(1, Z):
                v = v + C3[i][p].astype(F32)
            CF[i][z, :, lanes(y)] = v.astype(BF16)
            for p in range(1, Z):
                to = lax.rem(z + p, Z)
                mine = CF[i].at[z, :, lanes(y)]
                put(mine, mine, r.ccs.at[4 * i + 2], r.ccr.at[4 * i + 2], (to * 2 + y, c))

        def weights_back_y(i):
            take(CF[i].at[pl.ds(0, Z - 1), :, pl.ds(0, half_w)], r.ccr.at[4 * i + 2])
            mine = CF[i].at[:, :, lanes(y)]
            put(mine, mine, r.ccs.at[4 * i + 3], r.ccr.at[4 * i + 3], (ynb, c))

    G, GOR = r.gbe, r.gor
    take(GOR, r.gorr)

    @pl.loop(0, rows // BLK)
    def _(i):
        v = GO[k, block(i), :] + GOR[block(i), :]
        GOR[block(i), :] = v
        G[block(i, EDGE), :] = v.astype(BF16)

    put(G.at[pl.ds(EDGE, EDGE)], G.at[pl.ds(rows + EDGE, EDGE)], r.gs.at[0], r.gr.at[0], left_dev)
    put(G.at[pl.ds(rows, EDGE)], G.at[pl.ds(0, EDGE)], r.gs.at[1], r.gr.at[1], right_dev)
    GA, GP = r.ga, r.gp
    GA[EDGE : EDGE + rows, :] = nt(G[EDGE : EDGE + rows, :], mixf)

    def pull_two(at):
        v = normed2_of(CV[at, :])
        g = GA[at, :] * gelu_slope(v * gain2 + off2)
        GP[at, :] = g
        return g * v, g

    gs_, ss_ = lax.fori_loop(0, rows // BLK, row_sums(lambda i: pull_two(block(i, EDGE))), (zero_h, zero_h))
    spread(r.sa2, (gs_, ss_))
    sum_start(2)
    at(2)
    MP = r.mp
    mp = nn(r.a2t[...], G[EDGE : EDGE + rows, :]).astype(BF16).reshape(C, LANES, width)
    for p in range(C):
        MP[p % 2, p // 2] = mp[p, 0:cr, :]
    put(MP.at[1 - k], r.mr, r.mps.at[0], r.mpr.at[0], (s, other))
    at(3)
    sum_middle(2)
    HX = r.hbx
    take(HX, r.hbrem.at[0])
    HX[...] = HX[...] + HB[...]

    @pl.loop(1, S)
    def _(p):
        put(HX, r.hbf.at[s], r.hbsem.at[1], r.hbrem.at[1], (lax.rem(s + p, S), c))

    r.hbf[s] = HX[...]
    at(4)
    take(r.mr, r.mpr.at[0])
    MR = r.mr
    MR[...] = (MR[...].astype(F32) + MP[k].astype(F32)).astype(BF16)
    put(MR.at[xo], r.mx, r.mps.at[1], r.mpr.at[1], (s, xnb))
    at(5)
    take(r.xedge, r.gr.at[0])
    take(r.xedge, r.gr.at[1])
    for e in (0, rows + EDGE):
        GA[e : e + EDGE, :] = nt(G[e : e + EDGE, :], mixf)
        pull_two(slice(e, e + EDGE))
    at(6)
    total2, gsum2, ssum2 = sum_end(2, hp)
    r.tot[...] = total2
    r.g2[...] = r.tot[pl.ds(c, 1), 0:cr].reshape(cr)
    r.b2[...] = r.tot[pl.ds(C + c, 1), 0:cr].reshape(cr)
    coef2 = gain2 * scale2
    gmean2, smean2 = gsum2 * inv_bins, ssum2 * inv_bins
    GC, GB = r.gce, r.gcb

    def conv_grad(at):
        return (coef2 * (GP[at, :] - smean2 - normed2_of(CV[at, :]) * gmean2)).astype(BF16)

    hx = hp // 2

    @pl.loop(0, rows // BLK)
    def _(i):
        v = conv_grad(block(i, EDGE))
        GC[block(i, EDGE), :] = v.astype(F32)
        GB[0, block(i), :] = v[:, :hx]
        GB[1, block(i), :] = v[:, hx:]

    put(GB.at[xo], r.gcx, r.gbs, r.gbr, (s, xnb))
    take(r.mx, r.mpr.at[1])
    mix_sum = MR[xi].astype(F32) + r.mx[...].astype(F32)
    if fused:
        weights_out(0, mix_sum)
    else:
        r.mwg[...] = mix_sum
    GC[0:EDGE, :] = jnp.where(left_same, conv_grad(slice(0, EDGE)).astype(F32), 0.0)
    GC[rows + EDGE : ext, :] = jnp.where(right_same, conv_grad(slice(rows + EDGE, ext)).astype(F32), 0.0)
    at(7)


    G1 = r.ga1
    for t in range(TAPS):
        lo_t = EDGE + STEP - t * STEP
        part = nn(GC[lo_t : lo_t + rows, :].astype(BF16), CM[t].reshape(hp, width))
        G1[...] = part if t == 0 else G1[...] + part

    def pull_one(i):
        v = normed1_of(r.x[block(i), :].astype(F32))
        g = G1[block(i), :] * gelu_slope(v * gain1 + off1)
        G1[block(i), :] = g
        return g * v, g

    g1s, s1s = lax.fori_loop(0, rows // BLK, row_sums(pull_one), (zero_w, zero_w))
    spread(r.sa3, (g1s, s1s))
    sum_start(3)
    at(8)

    take(r.actx, r.ar_)
    take(r.gcx, r.gbr)
    ZP, CG = r.zpad, r.cg
    pad = ZP.shape[0] - rows
    ZP[0 : pad // 2, :] = jnp.zeros((pad // 2, hx), F32)
    ZP[rows + pad // 2 :, :] = jnp.zeros((pad // 2, hx), F32)
    for part in range(2):
        ZP[pad // 2 : pad // 2 + rows, :] = (GB[xi] if part == 0 else r.gcx[...]).astype(F32)
        rows_act = A[lo : lo + ext, :] if part == 0 else r.actx[...]
        for t in range(TAPS):
            lo_t = pad // 2 - EDGE + STEP - t * STEP
            v = nn(ZP[lo_t : lo_t + ext, :].T.astype(BF16), rows_act).reshape(2, LANES, width)
            CG[t] = v if part == 0 else CG[t] + v
    if fused:
        weights_along_z(0)
    put(CG.at[:, 1 - k, pl.ds(0, cr)], r.cgr, r.cgs, r.cgrr, (s, other))
    at(9)
    sum_middle(3)
    at(10)
    total1, gsum1, ssum1 = sum_end(3, width)
    r.g1[...] = gsum1.reshape(width)
    r.b1[...] = ssum1.reshape(width)
    coef1 = gain1 * scale1
    gmean1, smean1 = gsum1 * inv_bins, ssum1 * inv_bins

    @pl.loop(0, rows // BLK)
    def _(i):
        v = normed1_of(r.x[block(i), :].astype(F32))
        r.ig[block(i), :] = GOR[block(i), :] + coef1 * (G1[block(i), :] - smean1 - v * gmean1)

    at(11)

    take(r.cgr, r.cgrr)
    conv_sum = [CG[t, k, 0:cr, :] + r.cgr[t] for t in range(TAPS)]
    if fused:
        weights_out(1, jnp.concatenate([conv_sum[0], conv_sum[1][0:64]], axis=0))
        weights_out(2, jnp.concatenate([conv_sum[1][64:], conv_sum[2]], axis=0))
        at(12)
    else:
        for t in range(TAPS):
            r.cwg[t] = conv_sum[t]
        r.wgo[...] = WG[...]

    take(r.hbf.at[pl.ds(0, S - 1)], r.hbrem.at[1])
    HB3 = r.hb3
    HB3[...] = lax.fori_loop(1, S, lambda p, a: a + r.hbf[p], r.hbf[0])
    put(HB3, r.hbp, r.hbsem.at[2], r.hbrem.at[2], (s, other))
    at(13)

    if fused:
        weights_along_z(1)
        weights_along_z(2)
        at(14)
        weights_back_z(0)
        weights_back_z(1)
        weights_back_z(2)
        at(15)
        weights_back_y(0)
        weights_back_y(1)
        weights_back_y(2)
        at(16)
        for i in range(3):
            take(CF[i].at[:, :, pl.ds(0, half_w)], r.ccr.at[4 * i + 3])
        r.mwg[...] = CF[0][...].reshape(cr, width).astype(F32)
        v = CF[1][...].reshape(cr + 64, width).astype(F32)
        r.cwg[0] = v[0:cr]
        r.cwg[1, 0:64, :] = v[cr:]
        v = CF[2][...].reshape(2 * cr - 64, width).astype(F32)
        r.cwg[1, 64:, :] = v[0 : cr - 64]
        r.cwg[2] = v[cr - 64 :]
        at(17)
    take(r.hbp, r.hbrem.at[2])

    def in_order(dst, human, mouse):
        for m in range(M0 // HW):
            dst[:, m * HW : (m + 1) * HW] = human(m // NCHUNK, m % NCHUNK)
        edge = M0 // HW * HW
        v = human(edge // HALF_H, edge // HW % NCHUNK)
        if edge < M0:
            dst[:, edge:M0] = v[:, 0 : M0 - edge]
        before = v[:, M0 - edge : M0 - edge + LANES]
        lane = lax.broadcasted_iota(jnp.int32, (1, LANES), 1)
        for m in range(pl.cdiv(tracks - M0, LANES)):
            here = mouse(m // NCHUNK, m % NCHUNK) if m < 2 * NCHUNK else jnp.zeros_like(before)
            moved = pltpu.roll(here, OFF, 1)
            out = jnp.where(lane < OFF, before, moved)
            n = min(LANES, tracks - M0 - m * LANES)
            dst[:, M0 + m * LANES : M0 + m * LANES + n] = out[:, 0:n]
            before = moved

    HO = r.hbo
    HO[0] = jnp.where(k == 0, HB3[...], r.hbp[...])
    HO[1] = jnp.where(k == 0, r.hbp[...], HB3[...])
    in_order(r.hbrow, lambda h, j: HO[h, j : j + 1, 0:HW], lambda h, j: HO[h, j : j + 1, HW:CW])
    r.hb[...] = r.hbrow[...].reshape(tracks)
    if fused:
        for j in range(NCHUNK):
            take(r.fr.at[j], r.g4r.at[j])

        def piece(h, j, at, n):
            return jnp.where(k == h, r.fin[j, k, :, at : at + n], r.fr[j, :, at : at + n])

        in_order(r.hg, lambda h, j: piece(h, j, 0, HW), lambda h, j: piece(h, j, HW, MW))

    for i in range(4):
        take(r.ba[i].at[pl.ds(0, C - 1)], r.ars.at[2 * i])
        take(r.bb[i].at[pl.ds(0, S - 1)], r.ars.at[2 * i + 1])
    take(r.xl, r.hs.at[0])
    take(r.xr, r.hs.at[1])
    take(CM.at[0, 0, pl.ds(0, cr)], r.cms.at[0])
    take(CM.at[0, 0, pl.ds(0, cr), pl.ds(0, half_w)], r.cms.at[1])
    take(CS, r.cms.at[2])
    take(CM.at[0, 0, pl.ds(0, cr)], r.cms.at[3])
    take(CM.at[0, 0, pl.ds(0, cr)], r.cms.at[4])
    take(CM.at[0, 0, pl.ds(0, cr), pl.ds(0, half_w)], r.cms.at[5])
    take(CS, r.cms.at[6])
    take(r.gsb.at[pl.ds(0, C - 1)], r.gss)
    take(W.at[:, 0], r.wps)
    take(TG.at[:, 0], r.tps)
    take(W.at[:, pl.ds(0, 3), 0], r.wxs)
    take(W.at[:, pl.ds(0, 2), 0], r.wrs.at[0])
    take(W.at[:, pl.ds(0, 2), 0], r.wrs.at[1])
    take(W.at[:, 0, 0], r.wrs.at[2])
    take(r.actx, r.as_)
    take(O.at[0], r.os)
    take(GOR, r.gos)
    take(HX, r.hbsem.at[0])
    take(r.hbf.at[pl.ds(0, S - 1)], r.hbsem.at[1])
    take(HB3, r.hbsem.at[2])
    take(r.xedge, r.gs.at[0])
    take(r.xedge, r.gs.at[1])
    take(r.mr, r.mps.at[0])
    take(r.mx, r.mps.at[1])
    take(r.gcx, r.gbs)
    take(r.cgr, r.cgs)
    if fused:
        for i in range(3):
            take(C1[i], r.ccs.at[4 * i])
            take(C3[i].at[pl.ds(0, Z - 1)], r.ccs.at[4 * i + 1])
            take(CF[i].at[pl.ds(0, Z - 1), :, pl.ds(0, half_w)], r.ccs.at[4 * i + 2])
            take(CF[i].at[:, :, pl.ds(0, half_w)], r.ccs.at[4 * i + 3])
        for j in range(NCHUNK):
            take(R1.at[j], r.s1.at[j])
            take(R2.at[j], r.s2.at[j])
            take(R3.at[j, pl.ds(0, Z - 1)], r.s3.at[j])
            take(r.fr.at[j], r.s4.at[j])


def fused_step(seqs, chs, **ins):
    S, C = seqs, chs
    rows, width = ins["x"].shape
    n_dev = S * C
    hp = C * LANES
    cr = ins["mix"].shape[0]
    kr = ins["hw"].shape[1]
    tracks = ins["bias"].shape[0]
    ext = rows + 2 * EDGE
    Z = S // 2
    fused = width % (n_dev * 8) == 0 and Z == 4
    two = 2 * (width // n_dev)
    vm = pltpu.VMEM
    dma = pltpu.SemaphoreType.DMA
    any_ins = ("hw", "counts")
    outs = dict(
        out=((rows, width), BF16),
        ig=((rows, width), F32),
        g1=((width,), F32),
        b1=((width,), F32),
        cwg=((TAPS, cr, width), F32),
        g2=((cr,), F32),
        b2=((cr,), F32),
        mwg=((cr, width), F32),
        hb=((tracks,), F32),
    )
    if fused:
        outs["hg"] = ((two // 2, tracks), F32)
    else:
        outs["wgo"] = ((NCHUNK, Z, 2, 2, width // (4 * Z), HW), BF16)
    scratch = dict(
        xl=vm((HALO, width), BF16),
        xr=vm((HALO, width), BF16),
        xedge=vm((EDGE, width), BF16),
        gs2=vm((8, LANES), F32),
        gsb=vm((C, 8, LANES), F32),
        cm=vm((4, cr, width), BF16),
        cmf=vm((4, C, LANES, width), BF16),
        hwv=vm((4, kr, tracks), BF16),
        mwv=vm((4, kr, 2 * HALF_M), BF16),
        cbuf=vm((HUMAN, rows), jnp.int32),
        ctail=vm((HW - MW, rows), jnp.int32),
        hbpad=vm((1, HUMAN // LANES * LANES + (2 * NCHUNK + 1) * LANES), F32),
        bias_rows=vm((16, CW), F32),
        wbuf=vm((NCHUNK, 4, 4, kr, CW), BF16),
        tgb=vm((NCHUNK, 2, rows, HW), BF16),
        tgx=vm((NCHUNK, rows, HW), BF16),
        act=vm((rows + 2 * HALO, width), BF16),
        actx=vm((ext, width), BF16),
        prod=vm((TAPS, rows + 2 * HALO, hp), F32),
        cv=vm((ext, hp), F32),
        a2=vm((rows, hp), BF16),
        a2t=vm((hp, rows), BF16),
        ob=vm((2, rows, width), BF16),
        ot=vm((width, 2 * rows), BF16),
        wsel=vm((width, HW), BF16),
        lg=vm((2 * rows, HW), F32),
        gl=vm((2 * rows, HW), BF16),
        wg=vm((NCHUNK, Z, 2, 2, width // (4 * Z), HW), BF16),
        go=vm((2, rows, width), F32),
        gor=vm((rows, width), F32),
        hbs=vm((8, CW), F32),
        hbx=vm((8, CW), F32),
        hbf=vm((S, 8, CW), F32),
        hb3=vm((8, CW), F32),
        hbp=vm((8, CW), F32),
        hbo=vm((2, 8, CW), F32),
        hbrow=vm((1, tracks), F32),
        gbe=vm((ext, width), BF16),
        ga=vm((ext, hp), F32),
        gp=vm((ext, hp), F32),
        gce=vm((ext, hp), F32),
        gcb=vm((2, rows, hp // 2), BF16),
        gcx=vm((rows, hp // 2), BF16),
        ga1=vm((rows, width), F32),
        mp=vm((2, 2, cr, width), BF16),
        mr=vm((2, cr, width), BF16),
        mx=vm((cr, width), BF16),
        zpad=vm((rows + 64, hp // 2), F32),
        cg=vm((TAPS, 2, LANES, width), F32),
        cgr=vm((TAPS, cr, width), F32),
        tot=vm((8, LANES), F32),
    )
    for i, n in enumerate((16, 8, 8, 16)):
        scratch[f"sa{i}"] = vm((n, LANES), F32)
        scratch[f"sb{i}"] = vm((n, LANES), F32)
        scratch[f"ba{i}"] = vm((C, n, LANES), F32)
        scratch[f"bb{i}"] = vm((S, n, LANES), F32)
    sems = dict(
        ars=8, arr=8, hs=2, hr=2, cms=7, cmr=7, gss=0, gsr=0, ld=2, wl=7, wp=7, wx=7, wy=7, wz=7, wd=7, wps=0, wxs=0,
        wrs=3, tp=7, tps=0, as_=0, ar_=0, os=0, gos=0, gorr=0, hbsem=3, hbrem=3, gs=2, gr=2, mps=2, mpr=2, gbs=0,
        gbr=0, cgs=0, cgrr=0, orr=0,
    )
    if fused:
        scratch.update(
            acc1=vm((NCHUNK, Z, 2, two, CW), BF16),
            r1=vm((NCHUNK, Z, 2, two, HW), BF16),
            r2=vm((NCHUNK, Z, two, CW), BF16),
            r3=vm((NCHUNK, Z, two, CW), BF16),
            fin=vm((NCHUNK, 2, two // 2, CW), F32),
            fr=vm((NCHUNK, two // 2, CW), F32),
        )
        for i, n in enumerate((cr, cr + 64, 2 * cr - 64)):
            scratch[f"cp{i}"] = vm((Z, n // Z, width), BF16)
            scratch[f"c1{i}"] = vm((Z, n // Z, width // 2), BF16)
            scratch[f"c3{i}"] = vm((Z, n // Z, width // 2), BF16)
            scratch[f"cf{i}"] = vm((Z, n // Z, width), BF16)
        sems.update(s1=7, s2=7, s3=7, s4=7, g1r=7, g2r=7, g3r=7, g4r=7, ccs=12, ccr=12)
    for name, n in sems.items():
        scratch[name] = dma((n,)) if n else dma
    names = [*ins, *outs, *scratch]

    def space(name):
        if name == "species":
            return pl.BlockSpec(memory_space=pltpu.SMEM)
        return pl.BlockSpec(memory_space=pl.ANY if name in any_ins else pltpu.VMEM)

    got = pl.pallas_call(
        functools.partial(kernel_body, S, C, fused, names),
        out_shape=[jax.ShapeDtypeStruct(*v) for v in outs.values()],
        in_specs=[space(n) for n in ins],
        out_specs=[pl.BlockSpec(memory_space=pltpu.VMEM) for _ in outs],
        scratch_shapes=list(scratch.values()),
        compiler_params=pltpu.CompilerParams(
            collective_id=0, has_side_effects=True, vmem_limit_bytes=67_043_328
        ),
    )(*ins.values())
    return types.SimpleNamespace(**dict(zip(outs, got, strict=True))), fused


def handed_on(values):
    def body(*refs):
        n = len(values)
        sems = refs[2 * n]
        for i in range(n):
            pltpu.make_async_copy(refs[i], refs[n + i], sems.at[i]).start()
        for i in range(n):
            pltpu.make_async_copy(refs[i], refs[n + i], sems.at[i]).wait()

    return pl.pallas_call(
        body,
        out_shape=[jax.ShapeDtypeStruct(v.shape, v.dtype) for v in values],
        in_specs=[pl.BlockSpec(memory_space=pltpu.VMEM) for _ in values],
        out_specs=[pl.BlockSpec(memory_space=pl.ANY) for _ in values],
        scratch_shapes=[pltpu.SemaphoreType.DMA((len(values),))],
    )(*values)


def on_device(
    inputs, gain_one, shift_one, conv_weight, gain_two, shift_two, mix_weight, head_weight, head_bias, species, counts
):
    S, C = lax.axis_size("seq"), lax.axis_size("ch")
    s, c = lax.axis_index("seq"), lax.axis_index("ch")
    rows, width = inputs.shape
    depth, tracks = head_weight.shape
    o, fused = fused_step(
        S,
        C,
        x=inputs,
        gain1=gain_one,
        shift1=shift_one,
        cw=jnp.transpose(conv_weight, (0, 2, 1)),
        gain2=gain_two,
        shift2=shift_two,
        mix=mix_weight,
        hw=head_weight.reshape(4, depth // 4, tracks),
        bias=head_bias,
        species=species,
        counts=jnp.transpose(counts),
    )
    cwg, mwg = o.cwg, o.mwg
    if fused:
        head_weight_grad = o.hg
    else:
        cwg, mwg = lax.psum((cwg, mwg), "seq")
        part = o.wgo.reshape(NCHUNK, width, HW).astype(F32)
        part = jnp.transpose(part, (1, 0, 2))
        k = lax.rem(c, 2)
        human = jnp.zeros((width, 2, HALF_H), F32).at[:, k].set(part.reshape(width, HALF_H))
        mouse = jnp.zeros((width, 2, HALF_M), F32).at[:, k].set(part[:, :, :MW].reshape(width, HALF_M))
        first = (s * C + c // 2 * 2) * rows
        window = jnp.mod(first - SHIFT, rows * S * C) // WINDOW_BINS
        is_h = jnp.sum(jnp.where(jnp.arange(species.shape[0], dtype=jnp.int32) == window, species, 0)) == 0
        human = jnp.where(is_h, human.reshape(width, 2 * HALF_H)[:, :HUMAN], 0.0)
        mouse = jnp.where(is_h, 0.0, mouse.reshape(width, 2 * HALF_M)[:, :MOUSE])
        head_weight_grad = lax.psum_scatter(
            jnp.concatenate([human, mouse], axis=1), ("seq", "ch"), scatter_dimension=0, tiled=True
        )
    if fused:
        names = list(vars(o))
        o = types.SimpleNamespace(**dict(zip(names, handed_on(list(vars(o).values())), strict=True)))
        cwg, mwg, head_weight_grad = o.cwg, o.mwg, o.hg
    return (
        o.out,
        o.ig,
        o.g1,
        o.b1,
        jnp.transpose(cwg, (0, 2, 1)),
        o.g2,
        o.b2,
        mwg,
        head_weight_grad,
        o.hb,
    )


def solution(mesh):
    rows = P(("seq", "ch"), None)
    in_specs = (
        rows, P(), P(), P(None, None, "ch"), P("ch"), P("ch"), P("ch", None), P("ch", None), P(), P(), rows,
    )
    out_specs = (
        rows, rows, P(), P(), P(None, None, "ch"), P("ch"), P("ch"), P("ch", None), rows, P(),
    )
    return jax.shard_map(on_device, mesh=mesh, in_specs=in_specs, out_specs=out_specs, check_vma=False)
```

time: 175 us -> 134 us (0.77)
  local copies, waits for them, and re-layouts: 18.6 us -> 0 us
  other arithmetic: 15.3 us -> 0 us
  Pallas kernels: 140 us -> 133 us
    pallas_call x1, Pallas kernels: 140 us -> 130 us  [fused_step(): pl.pallas_call(functools.partial(kernel_body, S, C, fused, names), out_sh...]
    convert_element_type x1 -> x0, other arithmetic: 4.53 us -> none  [on_device(): tg = jnp.pad(counts.astype(BF16), ((0, 0), (0, 2 * HALF_H - HUMAN)))]
    another operation x3 -> x0, other arithmetic: 4.4 us -> none  [the longest x1 2.52 us: on_device(): jnp.stack([species_at(s, xi), species_at(s, 1 - xi), species_at(s + 1 - 2...]
    concatenate x4 -> x0, other arithmetic: 4.24 us -> none  [the longest x1 1.96 us: on_device(): jnp.concatenate([jnp.transpose(conv_weight, (0, 2, 1)), mix_weight[None]]...]
    pallas_call x0 -> x1, Pallas kernels: none -> 3.58 us  [handed_on(): pl.pallas_call(body, out_shape=[jax.ShapeDtypeStruct(v.shape, v.dtype) fo...]
    slice x7 -> x0, local copies, waits for them, and re-layouts: 3.52 us -> none  [the longest x1 1.38 us: on_device(): o.g1[1]]
    convert_element_type x1 -> x0, local copies, waits for them, and re-layouts: 3.3 us -> none  [on_device(): tg = jnp.pad(counts.astype(BF16), ((0, 0), (0, 2 * HALF_H - HUMAN)))]
    transpose x5 -> x0, local copies, waits for them, and re-layouts: 3.24 us -> none  [the longest x2 1.28 us: whole(): jnp.transpose(v[..., :HW], (2, 0, 1, 3)).reshape(n, 2 * HALF_H)[:, :HUMAN]]
where the time goes in v2:
time: 134 us
  Pallas kernels  133 us (99%)
    pallas_call x1, Pallas kernels, fused_step(): pl.pallas_call(functools.partial(kernel_body, S, C, fused, names), out_sh...  130 us
    pallas_call x1, Pallas kernels, handed_on(): pl.pallas_call(body, out_shape=[jax.ShapeDtypeStruct(v.shape, v.dtype) fo...  3.58 us

profile of v2, /device:TPU:1, one launch (start us, length us, event | category | flops | bytes accessed | tf_op | source)
XLA Modules:
  0.0 133.8 jit_solution(17273238503782546488)
XLA Ops:
  0.6 129.5 %shard_map.186 = (bf16[256,768]{1,0:T(8,128)(2,1)}, f32[256,768]{1,0:T(8,128)}, f32[768]{0:T(1024)}, f32[768]{0:T(1024)}, f32[3,96,768]{2,1,0:T(8,128)}, /*index...) custom-call(bf16[256,768]{1,0:T(8,128)(2,1)} %refs_0_.1, f32[768]{0:T(1024)} %refs_1_.1, ...), custom_call_target="tpu_custom_call" | custom-call | tf_op jit(solution)/shard_map/pallas_call | solution.py:985
  130.2 3.6 %shard_map.187 = (bf16[256,768]{1,0:T(8,128)(2,1)}, f32[256,768]{1,0:T(8,128)}, f32[768]{0:T(1024)}, f32[768]{0:T(1024)}, f32[3,96,768]{2,1,0:T(8,128)}, /*index...) custom-call(bf16[256,768]{1,0:T(8,128)(2,1)} %get-tuple-element.30.refs_0_, ...), custom_call_target="tpu_custom_call" | custom-call | tf_op jit(solution)/shard_map/pallas_call | solution.py:1007

commit v3 on v2

--- a/solution.py
+++ b/solution.py
@@ -34,20 +34,29 @@
 
 
 PLAN = {
-    0: ((0, 0),),
-    2: ((2, 4),),
-    4: ((2, 5),),
-    5: ((3, 2),),
-    7: ((2, 6),),
-    13: ((3, 3),),
-    14: ((3, 4),),
-    15: ((3, 5), (3, 6)),
-    16: ((4, 0), (4, 1), (4, 2), (4, 3)),
-    17: ((4, 4), (4, 5), (4, 6)),
+    100: ((6, 4), (6, 0), (6, 3)),
+    101: ((5, 4), (6, 1), (5, 0)),
+    102: ((5, 3),),
+    103: ((6, 2), (6, 5), (6, 6)),
+    104: ((5, 1), (5, 2), (0, 0)),
+    105: ((5, 5),),
+    110: ((5, 6),),
+    112: ((1, 1), (1, 0)),
+    114: ((1, 2),),
+    2: ((2, 1), (2, 2)),
+    5: ((1, 5),),
+    6: ((2, 0), (3, 1), (3, 2)),
+    8: ((3, 0), (1, 4), (2, 5)),
+    9: ((4, 1), (4, 2)),
+    10: ((1, 3),),
+    12: ((1, 6),),
+    13: ((3, 5),),
+    14: ((2, 4), (4, 0), (2, 3)),
+    15: ((2, 6), (4, 5), (3, 3), (3, 4)),
+    16: ((3, 6),),
+    17: ((4, 3), (4, 4), (4, 6)),
 }
-LOOP = ((0, 7), (3, 4), (5, 2))
-XFIRST = 3
-RELAYED = 5
+X_FIRST = (2, 3, 6)
 
 
 def nn(a, b):
@@ -316,8 +325,21 @@
             r.wrs.at[2], r.wd.at[j], (dnb, c),
         )
 
-    for j in range(XFIRST):
-        heads_along_x(j)
+    def at(slot):
+        for stage, j in PLAN.get(slot, ()):
+            if stage == 0:
+                put(A.at[pl.ds(HALO - EDGE, ext)], r.actx, r.as_, r.ar_, (s, xnb))
+            elif stage == 5:
+                relay_heads(j)
+            elif stage == 6:
+                heads_along_x(j)
+            elif fused and stage == 4:
+                last(j)
+            elif fused:
+                (first, second, third)[stage - 1](j, j in X_FIRST)
+
+    ext = rows + 2 * EDGE
+    at(100)
 
     def pass_weights():
         take(CM.at[0, 0, pl.ds(0, cr)], r.cmr.at[0])
@@ -380,7 +402,7 @@
     take(r.xr, r.hr.at[1])
     A[rows + HALO : rows + 2 * HALO, :] = jnp.where(right_same, act_rows(r.xr[...]), 0.0).astype(BF16)
 
-    relay_heads(0)
+    at(101)
     take(CM.at[0, 0, pl.ds(0, cr), pl.ds(0, half_w)], r.cmr.at[1])
     take(CM.at[0, 0, pl.ds(0, cr)], r.cmr.at[3])
     take(CM.at[0, 0, pl.ds(0, cr)], r.cmr.at[4])
@@ -389,7 +411,6 @@
     take(CM.at[:, 0, pl.ds(0, cr)], r.cmr.at[2])
     take(CM.at[:, 0, pl.ds(0, cr)], r.cmr.at[6])
 
-    ext = rows + 2 * EDGE
     PR = r.prod
     for t in range(TAPS):
         PR[t] = nt(A[...], CM[t].reshape(hp, width))
@@ -398,7 +419,7 @@
     CV[...] = (
         PR[0, lo - STEP : lo - STEP + ext, :] + PR[1, lo : lo + ext, :] + PR[2, lo + STEP : lo + STEP + ext, :]
     )
-    relay_heads(1)
+    at(102)
     zero_h = jnp.zeros((1, hp), F32)
 
     def c_terms(i):
@@ -408,8 +429,7 @@
     s2, q2 = lax.fori_loop(0, rows // BLK, row_sums(c_terms), (zero_h, zero_h))
     spread(r.sa1, (s2, q2))
     sum_start(1)
-    for j in range(XFIRST, NCHUNK):
-        heads_along_x(j)
+    at(103)
 
     @pl.loop(0, NCHUNK)
     def _(j):
@@ -417,7 +437,7 @@
         put(r.tgx.at[j], TG.at[j, k], r.tps, r.tp.at[j], (s, other))
 
     sum_middle(1)
-    relay_heads(2)
+    at(104)
     _, t2, u2 = sum_end(1, hp)
     mean2 = t2 * inv_bins
     scale2 = lax.rsqrt(u2 * inv_bins - mean2 * mean2 + EPS)
@@ -442,15 +462,14 @@
     O[k] = outputs
     r.out[...] = outputs
     put(O.at[k], O.at[k], r.os, r.orr, (s, other))
-    for j in range(3, RELAYED):
-        relay_heads(j)
+    at(105)
     r.a2t[...] = A2[...].T
     take(O.at[0], r.orr)
     OT = r.ot
     OT[...] = O[...].reshape(2 * rows, width).T
     GO = r.go
     GO[...] = jnp.zeros(GO.shape, F32)
-    WG, GL = r.wg, r.gl
+    WG, GL = r.wg, (r.gl0, r.gl1)
     LG = r.lg
     HB = r.hbs
     HB[...] = jnp.zeros(HB.shape, F32)
@@ -504,79 +523,53 @@
             r.fin[j] = v.reshape(2, own, CW)
             put(r.fin.at[j, 1 - k], r.fr.at[j], r.s4.at[j], r.g4r.at[j], (s, other))
 
-        def either(step, j):
-            @pl.when(lax.rem(j, 2) == 1)
-            def _():
-                step(j, True)
-
-            @pl.when(lax.rem(j, 2) == 0)
-            def _():
-                step(j, False)
-
-    def heads_chunk(j):
+    def chunk_arrives(j):
         take(W.at[j, 0], r.wl.at[j])
         take(W.at[j, 0], r.wp.at[j])
         take(W.at[j, pl.ds(0, 2), 0], r.wy.at[j])
         take(W.at[j, pl.ds(0, 2), 0], r.wz.at[j])
         take(W.at[j, pl.ds(0, 2), 0, :, pl.ds(0, HALFC)], r.wd.at[j])
         take(TG.at[j, 0], r.tp.at[j])
-        w = r.wsel
-        w[:, MW:] = W[j, :, :, :, MW:HW].reshape(width, HW - MW)
-        w[:, :MW] = jnp.where(
+
+    def tracks_of(j):
+        head = jnp.where(
             mine_h, W[j, :, :, :, 0:MW].reshape(width, MW), W[j, :, :, :, HW:CW].reshape(width, MW)
         )
-        wv = w[...]
-        LG[...] = nn(O[...].reshape(2 * rows, width), wv)
+        return jnp.concatenate([head, W[j, :, :, :, MW:HW].reshape(width, HW - MW)], axis=1)
+
+    def chunk_grads(j):
+        wv = tracks_of(j)
+        for h in range(2):
+            LG[h] = nn(O[h], wv)
         valid_n = jnp.where(mine_h, HUMAN - (k * HALF_H + j * HW), jnp.minimum(MOUSE - (k * HALF_M + j * MW), MW))
         valid = lax.broadcasted_iota(jnp.int32, (1, HW), 1) < valid_n
         brow = BR[pl.ds(k * NCHUNK + j, 1), :]
         bias = jnp.concatenate([jnp.where(mine_h, brow[:, :MW], brow[:, HW:]), brow[:, MW:HW]], axis=1)
-        per = rows // BLK
-
-        def step(i, acc):
-            at = pl.multiple_of(i * BLK, BLK)
-            core = i // per
-            ta = pl.ds(pl.multiple_of(lax.rem(i, per) * BLK, BLK), BLK)
-            lg = LG[pl.ds(at, BLK), :] + bias
-            tgt = TG[j, core, ta, :].astype(F32)
-            g = jnp.where(valid, poisson_grad(lg, tgt), 0.0).astype(BF16)
-            GL[pl.ds(at, BLK), :] = g
-            return acc + jnp.sum(g.astype(F32).reshape(BLK // 8, 8, HW), 0)
-
-        bsum = jnp.sum(lax.fori_loop(0, 2 * per, step, jnp.zeros((8, HW), F32)), 0, keepdims=True)
-        bsum = jnp.concatenate([jnp.where(mine_h, bsum, 0.0), jnp.where(mine_h, 0.0, bsum[:, :MW])], axis=1)
-        HB[...] = jnp.where(lax.broadcasted_iota(jnp.int32, HB.shape, 0) == j, bsum, HB[...])
-        g = GL[...]
-        GO[...] += nt(g, wv).reshape(GO.shape)
+        acc = jnp.zeros((8, HW), F32)
+        for h in range(2):
+            for i in range(rows // BLK):
+                at = slice(i * BLK, (i + 1) * BLK)
+                g = poisson_grad(LG[h, at, :] + bias, TG[j, h, at, :].astype(F32))
+                g = jnp.where(valid, g, 0.0).astype(BF16)
+                GL[j % 2][h, at, :] = g
+                acc = acc + jnp.sum(g.astype(F32).reshape(BLK // 8, 8, HW), 0)
+        bsum = jnp.sum(acc, 0, keepdims=True)
+        HB[j : j + 1, 0:HW] = jnp.where(mine_h, bsum, 0.0)
+        HB[j : j + 1, HW:CW] = jnp.where(mine_h, 0.0, bsum[:, :MW])
+
+    def chunk_products(j):
+        g = GL[j % 2][...].reshape(2 * rows, HW)
+        GO[...] += nt(g, tracks_of(j)).reshape(GO.shape)
         WG[j] = nn(OT[...], g).astype(BF16).reshape(WG.shape[1:])
 
-    act_rows_out = functools.partial(put, A.at[pl.ds(lo, ext)], r.actx, r.as_, r.ar_, (s, xnb))
-
-    def at(slot):
-        for stage, j in PLAN.get(slot, ()):
-            if stage == 0:
-                act_rows_out()
-            elif fused:
-                (first, second, third)[stage - 1](j, j % 2 == 1) if stage < 4 else last(j)
-
     at(0)
-
-    @pl.loop(0, NCHUNK)
-    def _(j):
-        heads_chunk(j)
-
-        @pl.when(j + RELAYED < NCHUNK)
-        def _():
-            relay_heads(j + RELAYED)
-
-        if fused:
-            for stage, step in ((1, first), (2, second), (3, third)):
-                lag, count = LOOP[stage - 1]
-                if count > 0:
-
-                    @pl.when((j >= lag) & (j - lag < count))
-                    def _(step=step, lag=lag):
-                        either(step, j - lag)
+    for j in range(NCHUNK + 1):
+        if j < NCHUNK:
+            chunk_arrives(j)
+            chunk_grads(j)
+        if j > 0:
+            chunk_products(j - 1)
+        at(110 + j)
 
     put(GO.at[1 - k], r.gor, r.gos, r.gorr, (s, other))
     put(r.hbs, r.hbx, r.hbsem.at[0], r.hbrem.at[0], (s, xnb))
@@ -717,38 +710,26 @@
     sum_start(3)
     at(8)
 
-    take(r.actx, r.ar_)
-    take(r.gcx, r.gbr)
     ZP, CG = r.zpad, r.cg
     pad = ZP.shape[0] - rows
     ZP[0 : pad // 2, :] = jnp.zeros((pad // 2, hx), F32)
     ZP[rows + pad // 2 :, :] = jnp.zeros((pad // 2, hx), F32)
     for part in range(2):
+        if part == 1:
+            take(r.actx, r.ar_)
+            take(r.gcx, r.gbr)
         ZP[pad // 2 : pad // 2 + rows, :] = (GB[xi] if part == 0 else r.gcx[...]).astype(F32)
         rows_act = A[lo : lo + ext, :] if part == 0 else r.actx[...]
         for t in range(TAPS):
             lo_t = pad // 2 - EDGE + STEP - t * STEP
             v = nn(ZP[lo_t : lo_t + ext, :].T.astype(BF16), rows_act).reshape(2, LANES, width)
             CG[t] = v if part == 0 else CG[t] + v
-    if fused:
-        weights_along_z(0)
     put(CG.at[:, 1 - k, pl.ds(0, cr)], r.cgr, r.cgs, r.cgrr, (s, other))
     at(9)
+    if fused:
+        weights_along_z(0)
     sum_middle(3)
     at(10)
-    total1, gsum1, ssum1 = sum_end(3, width)
-    r.g1[...] = gsum1.reshape(width)
-    r.b1[...] = ssum1.reshape(width)
-    coef1 = gain1 * scale1
-    gmean1, smean1 = gsum1 * inv_bins, ssum1 * inv_bins
-
-    @pl.loop(0, rows // BLK)
-    def _(i):
-        v = normed1_of(r.x[block(i), :].astype(F32))
-        r.ig[block(i), :] = GOR[block(i), :] + coef1 * (G1[block(i), :] - smean1 - v * gmean1)
-
-    at(11)
-
     take(r.cgr, r.cgrr)
     conv_sum = [CG[t, k, 0:cr, :] + r.cgr[t] for t in range(TAPS)]
     if fused:
@@ -766,9 +747,22 @@
     put(HB3, r.hbp, r.hbsem.at[2], r.hbrem.at[2], (s, other))
     at(13)
 
+    def input_gradient():
+        total1, gsum1, ssum1 = sum_end(3, width)
+        r.g1[...] = gsum1.reshape(width)
+        r.b1[...] = ssum1.reshape(width)
+        coef1 = gain1 * scale1
+        gmean1, smean1 = gsum1 * inv_bins, ssum1 * inv_bins
+
+        @pl.loop(0, rows // BLK)
+        def _(i):
+            v = normed1_of(r.x[block(i), :].astype(F32))
+            r.ig[block(i), :] = GOR[block(i), :] + coef1 * (G1[block(i), :] - smean1 - v * gmean1)
+
     if fused:
         weights_along_z(1)
         weights_along_z(2)
+        input_gradient()
         at(14)
         weights_back_z(0)
         weights_back_z(1)
@@ -788,6 +782,8 @@
         r.cwg[1, 64:, :] = v[0 : cr - 64]
         r.cwg[2] = v[cr - 64 :]
         at(17)
+    if not fused:
+        input_gradient()
     take(r.hbp, r.hbrem.at[2])
 
     def in_order(dst, human, mouse):
@@ -920,9 +916,9 @@
         a2t=vm((hp, rows), BF16),
         ob=vm((2, rows, width), BF16),
         ot=vm((width, 2 * rows), BF16),
-        wsel=vm((width, HW), BF16),
-        lg=vm((2 * rows, HW), F32),
-        gl=vm((2 * rows, HW), BF16),
+        lg=vm((2, rows, HW), F32),
+        gl0=vm((2, rows, HW), BF16),
+        gl1=vm((2, rows, HW), BF16),
         wg=vm((NCHUNK, Z, 2, 2, width // (4 * Z), HW), BF16),
         go=vm((2, rows, width), F32),
         gor=vm((rows, width), F32),

time: 134 us -> 115 us (0.86)
  Pallas kernels: 133 us -> 114 us
    pallas_call x1, Pallas kernels: 130 us -> 110 us  [fused_step(): pl.pallas_call(functools.partial(kernel_body, S, C, fused, names), out_sh...]
where the time goes in v3:
time: 115 us
  Pallas kernels  114 us (99%)
    pallas_call x1, Pallas kernels, fused_step(): pl.pallas_call(functools.partial(kernel_body, S, C, fused, names), out_sh...  110 us
    pallas_call x1, Pallas kernels, handed_on(): pl.pallas_call(body, out_shape=[jax.ShapeDtypeStruct(v.shape, v.dtype) fo...  3.58 us

profile of v3, /device:TPU:1, one launch (start us, length us, event | category | flops | bytes accessed | tf_op | source)
XLA Modules:
  0.0 114.8 jit_solution(17485233601657042336)
XLA Ops:
  0.6 110.4 %shard_map.186 = (bf16[256,768]{1,0:T(8,128)(2,1)}, f32[256,768]{1,0:T(8,128)}, f32[768]{0:T(1024)}, f32[768]{0:T(1024)}, f32[3,96,768]{2,1,0:T(8,128)}, /*index...) custom-call(bf16[256,768]{1,0:T(8,128)(2,1)} %refs_0_.1, f32[768]{0:T(1024)} %refs_1_.1, ...), custom_call_target="tpu_custom_call" | custom-call | tf_op jit(solution)/shard_map/pallas_call | solution.py:981
  111.0 3.6 %shard_map.187 = (bf16[256,768]{1,0:T(8,128)(2,1)}, f32[256,768]{1,0:T(8,128)}, f32[768]{0:T(1024)}, f32[768]{0:T(1024)}, f32[3,96,768]{2,1,0:T(8,128)}, /*index...) custom-call(bf16[256,768]{1,0:T(8,128)(2,1)} %get-tuple-element.30.refs_0_, ...), custom_call_target="tpu_custom_call" | custom-call | tf_op jit(solution)/shard_map/pallas_call | solution.py:1003

commit v4 on v3

--- a/solution.py
+++ b/solution.py
@@ -35,8 +35,8 @@
 
 PLAN = {
     100: ((6, 4), (6, 0), (6, 3)),
-    101: ((5, 4), (6, 1), (5, 0)),
-    102: ((5, 3),),
+    101: ((5, 4), (6, 1)),
+    102: ((5, 0), (5, 3)),
     103: ((6, 2), (6, 5), (6, 6)),
     104: ((5, 1), (5, 2), (0, 0)),
     105: ((5, 5),),
@@ -992,20 +992,27 @@
 
 
 def handed_on(values):
+    n = len(values)
+
     def body(*refs):
-        n = len(values)
-        sems = refs[2 * n]
+        ins, outs, held = refs[:n], refs[n : 2 * n], refs[2 * n : 3 * n]
+        come = [pltpu.make_async_copy(ins[i], held[i], refs[3 * n].at[i]) for i in range(n)]
+        go = [pltpu.make_async_copy(held[i], outs[i], refs[3 * n + 1].at[i]) for i in range(n)]
+        for copy in come:
+            copy.start()
         for i in range(n):
-            pltpu.make_async_copy(refs[i], refs[n + i], sems.at[i]).start()
-        for i in range(n):
-            pltpu.make_async_copy(refs[i], refs[n + i], sems.at[i]).wait()
+            come[i].wait()
+            go[i].start()
+        for copy in go:
+            copy.wait()
 
     return pl.pallas_call(
         body,
         out_shape=[jax.ShapeDtypeStruct(v.shape, v.dtype) for v in values],
-        in_specs=[pl.BlockSpec(memory_space=pltpu.VMEM) for _ in values],
+        in_specs=[pl.BlockSpec(memory_space=pl.ANY) for _ in values],
         out_specs=[pl.BlockSpec(memory_space=pl.ANY) for _ in values],
-        scratch_shapes=[pltpu.SemaphoreType.DMA((len(values),))],
+        scratch_shapes=[pltpu.VMEM(v.shape, v.dtype) for v in values]
+        + [pltpu.SemaphoreType.DMA((n,)), pltpu.SemaphoreType.DMA((n,))],
     )(*values)
 
 

time: 115 us -> 114 us (level)
  no operation moved by 1% of the time
where the time goes in v4:
time: 114 us
  Pallas kernels  113 us (99%)
    pallas_call x1, Pallas kernels, fused_step(): pl.pallas_call(functools.partial(kernel_body, S, C, fused, names), out_sh...  110 us
    pallas_call x1, Pallas kernels, handed_on(): pl.pallas_call(body, out_shape=[jax.ShapeDtypeStruct(v.shape, v.dtype) fo...  2.97 us

profile of v4, /device:TPU:1, one launch (start us, length us, event | category | flops | bytes accessed | tf_op | source)
XLA Modules:
  0.0 114.2 jit_solution(1531030254504788594)
XLA Ops:
  0.6 110.4 %shard_map.186 = (bf16[256,768]{1,0:T(8,128)(2,1)}, f32[256,768]{1,0:T(8,128)}, f32[768]{0:T(1024)}, f32[768]{0:T(1024)}, f32[3,96,768]{2,1,0:T(8,128)}, /*index...) custom-call(bf16[256,768]{1,0:T(8,128)(2,1)} %refs_0_.1, f32[768]{0:T(1024)} %refs_1_.1, ...), custom_call_target="tpu_custom_call" | custom-call | tf_op jit(solution)/shard_map/pallas_call | solution.py:981
  111.0 3.0 %shard_map.187 = (bf16[256,768]{1,0:T(8,128)(2,1)}, f32[256,768]{1,0:T(8,128)}, f32[768]{0:T(1024)}, f32[768]{0:T(1024)}, f32[3,96,768]{2,1,0:T(8,128)}, /*index...) custom-call(bf16[256,768]{1,0:T(8,128)(2,1)} %get-tuple-element.30.refs_0_, ...), custom_call_target="tpu_custom_call" | custom-call | tf_op jit(solution)/shard_map/pallas_call | solution.py:1009

commit v5 on v4

--- a/solution.py
+++ b/solution.py
@@ -47,9 +47,8 @@
     5: ((1, 5),),
     6: ((2, 0), (3, 1), (3, 2)),
     8: ((3, 0), (1, 4), (2, 5)),
-    9: ((4, 1), (4, 2)),
-    10: ((1, 3),),
-    12: ((1, 6),),
+    9: ((1, 3), (4, 1), (4, 2)),
+    10: ((1, 6),),
     13: ((3, 5),),
     14: ((2, 4), (4, 0), (2, 3)),
     15: ((2, 6), (4, 5), (3, 3), (3, 4)),

time: 114 us -> 114 us (level)
  no operation moved by 1% of the time
where the time goes in v5:
time: 114 us
  Pallas kernels  113 us (99%)
    pallas_call x1, Pallas kernels, fused_step(): pl.pallas_call(functools.partial(kernel_body, S, C, fused, names), out_sh...  110 us
    pallas_call x1, Pallas kernels, handed_on(): pl.pallas_call(body, out_shape=[jax.ShapeDtypeStruct(v.shape, v.dtype) fo...  2.97 us

profile of v5, /device:TPU:1, one launch (start us, length us, event | category | flops | bytes accessed | tf_op | source)
XLA Modules:
  0.0 114.2 jit_solution(2040878357496521895)
XLA Ops:
  0.6 110.4 %shard_map.186 = (bf16[256,768]{1,0:T(8,128)(2,1)}, f32[256,768]{1,0:T(8,128)}, f32[768]{0:T(1024)}, f32[768]{0:T(1024)}, f32[3,96,768]{2,1,0:T(8,128)}, /*index...) custom-call(bf16[256,768]{1,0:T(8,128)(2,1)} %refs_0_.1, f32[768]{0:T(1024)} %refs_1_.1, ...), custom_call_target="tpu_custom_call" | custom-call | tf_op jit(solution)/shard_map/pallas_call | solution.py:980
  111.0 3.0 %shard_map.187 = (bf16[256,768]{1,0:T(8,128)(2,1)}, f32[256,768]{1,0:T(8,128)}, f32[768]{0:T(1024)}, f32[768]{0:T(1024)}, f32[3,96,768]{2,1,0:T(8,128)}, /*index...) custom-call(bf16[256,768]{1,0:T(8,128)(2,1)} %get-tuple-element.30.refs_0_, ...), custom_call_target="tpu_custom_call" | custom-call | tf_op jit(solution)/shard_map/pallas_call | solution.py:1008
